TPU v7x, 256 devices: a whole 4x4x8 slice. The times are simulated.
256 devices in a mesh: lon: 16 (over x, y), lat: 16 (over z, core).
Axes of the slice: x: 4, y: 4, z: 8, core: 2. Of those that a mesh axis runs over, the one named last changes fastest.
Arguments:
- meridional_speed: float32 [16, 1024, 4096], P(None, 'lat', 'lon'), may hold values from -6 to 6
- theta_field: float32 [16, 1024, 4096], P(None, 'lat', 'lon'), may hold values from -2 to 30
- tier_vertical_span: float32 [16], replicated, may hold values from 0.5 to 4
- grid_zonal_span: float32 [1024, 4096], P('lat', 'lon'), may hold values from 0.05 to 40
- grid_plan_extent: float32 [1024, 4096], P('lat', 'lon'), may hold values from 0.2 to 5
- ocean_energy_input: float32 [1024, 4096], P('lat', 'lon'), may hold values from -6 to 6
- ocean_tier_tally: int32 [1024, 4096], P('lat', 'lon'), may hold values from 0 to 16, as said below
- grid_region_label: int32 [1024, 4096], P('lat', 'lon'), may hold values from 0 to 3
- seam_matching_meridian: int32 [4096], P('lon'), may hold values from 0 to 4095, as said below
Outputs:
- class_transport: float32 [4, 1024, 128], P(None, 'lat')
- overturning: float32 [4, 1024, 16], P(None, 'lat')
- heat_transport: float32 [4, 1024], P(None, 'lat')
- implied_transport: float32 [4, 1024], P(None, 'lat')
Inputs may be any that keep to these rules, and one draw needn't show every extreme that they name: `ocean_tier_tally`: one column, the same at every latitude, has at least one wet level, and every column of the northernmost row has at least one. seam_matching_meridian[i] = (c - i) mod 4096 for a c that each draw picks.
All inputs are finite; a program needn't handle non-finite values.
Results may differ from a plain program's by a relative error of at most 0.0003.
Values sent between devices are 32-bit elements; how exact they have to be, the bound alone decides.
A program may use at most 64 MiB of HBM per device.

v0:
```python
import math

import jax
import jax.numpy as jnp
from jax import lax
from jax.sharding import PartitionSpec as P

THERMAL_BINS = 128
OCEAN_REGIONS = 4


THERMAL_FLOOR = -2.0
THERMAL_RANGE = 32.0


def copy_for_each(array, axis):
    copies = jnp.broadcast_to(array, (lax.axis_size(axis), *array.shape))
    return lax.all_to_all(copies, axis, split_axis=0, concat_axis=0, tiled=True)


def folded_in_pairs(pieces, combine):
    while len(jax.tree.leaves(pieces)[0]) > 1:
        pieces = jax.vmap(combine)(*(pieces[side::2] for side in (0, 1)))
    return pieces[0]


def prefix(array, axis, combine, identity):
    devices, index = (lax.axis_size(axis), lax.axis_index(axis))
    passed = jnp.arange(devices) < index

    def kept(part, zero, own):
        part = jnp.where(
            passed.reshape(-1, *(1 for _ in own.shape)), part, jnp.asarray(zero, own.dtype)
        )
        return part

    pieces = copy_for_each(array, axis)
    return folded_in_pairs(kept(pieces, identity, array), combine)


def passed_along(block, axis, distance):
    devices = range(lax.axis_size(axis))
    route = [(i - distance, i) for i in devices if i - distance in devices]
    return lax.ppermute(block, axis, route)


def in_order(parts, dim):
    parts = jnp.moveaxis(parts, 0, dim)
    dims = parts.shape
    return parts.reshape(*dims[:dim], dims[dim] * dims[dim + 1], *dims[dim + 2 :])


def gathered_copies(array, axis, dim):
    return in_order(copy_for_each(array, axis), dim)


def taken_together(array, axis):
    everything = copy_for_each(array, axis)
    return jnp.sum(everything, axis=0)


def packed_total(arrays, axis):
    ends = [0]
    for a in arrays:
        ends.append(ends[-1] + a.size)
    so_far = taken_together(jnp.concatenate([a.ravel() for a in arrays]), axis)
    return tuple((so_far[b:e].reshape(a.shape) for a, b, e in zip(arrays, ends, ends[1:])))


def theta_bucket_edges(
    mass_conveyance, bucket_membership, lower_real_value, upper_interp_factor, theta_bucket_tally
):
    tier_ordinal, parallel_tally, meridian_tally = mass_conveyance.shape
    region_tally = bucket_membership.shape[0]
    block_rows = math.gcd(parallel_tally, 8)
    blocks = parallel_tally // block_rows

    def split_rows(array):
        lead = array.shape[0]
        return jnp.transpose(array.reshape(lead, blocks, block_rows, meridian_tally), (1, 0, 2, 3))

    def one_block(pieces):
        trans_blk, member_blk, low_blk, weight_blk = pieces
        theta_buckets = lax.broadcasted_iota(jnp.int32, (1, 1, 1, theta_bucket_tally), 3).astype(
            jnp.float32
        )
        low_cols = low_blk[..., None]
        weight_cols = weight_blk[..., None]
        tent = jnp.where(theta_buckets == low_cols, 1.0 - weight_cols, 0.0) + jnp.where(
            theta_buckets == low_cols + 1.0, weight_cols, 0.0
        )
        weighted = member_blk[:, None, :, :] * trans_blk[None, :, :, :]
        return jnp.einsum("bkri,krim->brm", weighted, tent, precision=lax.Precision.HIGHEST)

    binned = lax.map(
        one_block,
        (
            split_rows(mass_conveyance),
            split_rows(bucket_membership),
            split_rows(lower_real_value),
            split_rows(upper_interp_factor),
        ),
    )
    return jnp.transpose(binned, (1, 0, 2, 3)).reshape(
        region_tally, parallel_tally, theta_bucket_tally
    )


def vertical_aggregate_field(
    meridional_speed,
    theta_field,
    tier_vertical_span,
    grid_zonal_span,
    grid_plan_extent,
    ocean_energy_input,
    ocean_tier_tally,
    grid_region_label,
    subsequent_theta,
    subsequent_vertical_extent,
    theta_bucket_tally,
    region_tally,
):
    tier_ordinal, parallel_tally, meridian_tally = theta_field.shape
    poleward_theta = jnp.concatenate([theta_field[:, 1:, :], subsequent_theta[:, None, :]], axis=1)
    interface_theta = 0.5 * (theta_field + poleward_theta)
    north_depth = jnp.concatenate(
        [ocean_tier_tally[1:, :], subsequent_vertical_extent[None, :]], axis=0
    )
    face_depth = jnp.minimum(ocean_tier_tally, north_depth)
    level_iota = lax.broadcasted_iota(jnp.int32, (tier_ordinal, 1, 1), 0)
    wet_mask = (level_iota < face_depth[None, :, :]).astype(jnp.float32)
    water_capacity = wet_mask * tier_vertical_span[:, None, None] * grid_zonal_span[None, :, :]
    mass_conveyance = water_capacity * meridional_speed
    bucket_spacing = THERMAL_RANGE / theta_bucket_tally
    placement_offset = jnp.clip(
        (interface_theta - THERMAL_FLOOR) / bucket_spacing, 0.0, theta_bucket_tally - 1.0
    )
    lower_real_value = jnp.minimum(jnp.floor(placement_offset), theta_bucket_tally - 2.0)
    upper_interp_factor = placement_offset - lower_real_value
    basin_iota = lax.broadcasted_iota(jnp.int32, (region_tally, 1, 1), 0)
    bucket_membership = (grid_region_label[None, :, :] == basin_iota).astype(jnp.float32)
    bucket_aggregate = theta_bucket_edges(
        mass_conveyance,
        bucket_membership,
        lower_real_value,
        upper_interp_factor,
        theta_bucket_tally,
    )
    level_sum = jnp.einsum(
        "bji,kji->bjk", bucket_membership, mass_conveyance, precision=lax.Precision.HIGHEST
    )
    energy_aggregate = jnp.einsum(
        "dwk,wk->dw",
        bucket_membership,
        jnp.sum(mass_conveyance * interface_theta, axis=0),
        precision=lax.Precision.HIGHEST,
    )
    parallel_theta_field = jnp.sum(water_capacity * interface_theta, axis=(0, 2))
    row_wet = jnp.sum(water_capacity, axis=(0, 2))
    flux_rows = jnp.einsum(
        "dwk,wk->dw",
        bucket_membership,
        ocean_energy_input * grid_plan_extent,
        precision=lax.Precision.HIGHEST,
    )
    return (bucket_aggregate, level_sum, energy_aggregate, parallel_theta_field, row_wet, flux_rows)


def finish_rows(
    bucket_aggregate, level_sum, energy_aggregate, parallel_theta_field, row_wet, unit_scale
):
    row_mean = parallel_theta_field / row_wet
    volume_total = jnp.sum(level_sum, axis=2)
    heat_out = unit_scale / 16.0 * (energy_aggregate - volume_total * row_mean[None, :])
    stream = unit_scale * jnp.cumsum(level_sum, axis=2)
    return (unit_scale * bucket_aggregate, stream, heat_out)


def combine_sum(earlier, later):
    return earlier + later


def south_offset(totals):
    return prefix(totals, "lat", combine_sum, jnp.zeros_like(totals))


def body(
    meridional_speed,
    theta_field,
    tier_vertical_span,
    grid_zonal_span,
    grid_plan_extent,
    ocean_energy_input,
    ocean_tier_tally,
    grid_region_label,
    seam_matching_meridian,
):
    tier_ordinal, parallel_tally, meridian_tally = theta_field.shape
    lon_size = lax.axis_size("lon")
    lat_size = lax.axis_size("lat")
    width_total = meridian_tally * lon_size
    height_total = parallel_tally * lat_size
    unit_scale = math.sqrt(THERMAL_BINS / (width_total * tier_ordinal))
    implied_scale = 2.0 / math.sqrt(width_total * height_total)
    equatorward_limit_value = (theta_field[:, 0, :], ocean_tier_tally[0, :].astype(jnp.float32))
    upper_theta_value, above_depth = passed_along(
        (equatorward_limit_value[0], equatorward_limit_value[1]), "lat", -1
    )
    fold_edge = (
        theta_field[:, parallel_tally - 1, :],
        ocean_tier_tally[parallel_tally - 1, :].astype(jnp.float32),
    )
    seam_theta, fold_depth = (
        gathered_copies(fold_edge[0], "lon", 1),
        gathered_copies(fold_edge[1], "lon", 0),
    )
    reflected_theta = jnp.take(seam_theta, seam_matching_meridian, axis=1)
    mirror_depth = jnp.take(fold_depth, seam_matching_meridian, axis=0)
    on_seam_flag = lax.axis_index("lat") == lat_size - 1
    subsequent_theta = jnp.where(on_seam_flag, reflected_theta, upper_theta_value)
    subsequent_vertical_extent = jnp.where(on_seam_flag, mirror_depth, above_depth).astype(
        jnp.int32
    )
    bucket_aggregate, level_sum, energy_aggregate, parallel_theta_field, row_wet, flux_rows = (
        vertical_aggregate_field(
            meridional_speed,
            theta_field,
            tier_vertical_span,
            grid_zonal_span,
            grid_plan_extent,
            ocean_energy_input,
            ocean_tier_tally,
            grid_region_label,
            subsequent_theta,
            subsequent_vertical_extent,
            THERMAL_BINS,
            OCEAN_REGIONS,
        )
    )
    summed = packed_total(
        (bucket_aggregate, level_sum, energy_aggregate, parallel_theta_field, row_wet, flux_rows),
        "lon",
    )
    class_out, stream, heat_out = finish_rows(
        summed[0], summed[1], summed[2], summed[3], summed[4], unit_scale
    )
    flux_total = summed[5]
    late_offset = south_offset(jnp.sum(flux_total, axis=1))
    implied = implied_scale * (late_offset[:, None] + jnp.cumsum(flux_total, axis=1))
    return (class_out, stream, heat_out, implied)


def solution(mesh):
    in_specs = (
        P(None, "lat", "lon"),
        P(None, "lat", "lon"),
        P(),
        P("lat", "lon"),
        P("lat", "lon"),
        P("lat", "lon"),
        P("lat", "lon"),
        P("lat", "lon"),
        P("lon"),
    )
    out_specs = (P(None, "lat", None), P(None, "lat", None), P(None, "lat"), P(None, "lat"))
    return jax.shard_map(body, mesh=mesh, in_specs=in_specs, out_specs=out_specs, check_vma=False)
```

profile of v0, /device:TPU:1, one launch (start us, length us, event | category | flops | bytes accessed | tf_op | source)
XLA Modules:
  0.0 321.6 jit_solution(11539599296509700534)
XLA Ops:
  1.4 5.1 %collective-permute-start.1 = (f32[256]{0:T(256)S(1)}, f32[256]{0:T(256)S(1)}, u32[]{:S(2)}, u32[]{:S(2)}) collective-permute-start(f32[256]{0:T(256)S(1)} %bitcast.84), channel_id=1, source_target_pairs={{1,0},{2,1},{3,2},{4,3},{5,4},{6,5},{7,6},{8,7},{9,8},{10,9},{11,1... | collective-permute-start | bytes 3080 | tf_op jit(solution)/shard_map/ppermute | solution.py:44
  7.1 5.0 %all-to-all-start.1 = ((f32[16,1,256]{2,1,0:T(1,128)}), f32[16,1,256]{2,1,0:T(1,128)S(1)}, u32[]{:S(2)}, u32[]{:S(2)}) async-start(f32[16,1,256]{2,1,0:T(1,128)} %broadcast_in_dim.90), calls=%async_computation.1 | async-start | bytes 32768 | tf_op jit(solution)/shard_map/all_to_all | solution.py:18
  13.2 1.9 collective-permute-start
  22.6 6.8 %all-to-all-start = ((f32[16,16,256]{2,1,0:T(8,128)}), f32[16,16,256]{2,1,0:T(8,128)S(1)}, u32[]{:S(2)}, u32[]{:S(2)}) async-start(f32[16,16,256]{2,1,0:T(8,128)} %broadcast_in_dim.86), calls=%async_computation | async-start | bytes 524288 | tf_op jit(solution)/shard_map/all_to_all | solution.py:18
  29.4 1.7 gather_fusion.1
  31.2 6.7 %all-to-all-done = f32[16,16,256]{2,1,0:T(8,128)S(1)} async-done(((f32[16,16,256]{2,1,0:T(8,128)}), f32[16,16,256]{2,1,0:T(8,128)S(1)}, u32[]{:S(2)}, u32[]{:S(2)}) %all-to-all-start) | async-done | bytes 262176 | tf_op jit(solution)/shard_map/all_to_all | solution.py:18
  38.0 2.0 copy.57
  39.9 2.3 gather_fusion
  42.4 2.4 multiply_reduce_fusion
  50.1 208.4 %while.10 = (s32[]{:T(128)}, f32[8,4,8,128]{3,2,0,1:T(8,128)S(1)}, f32[8,16,8,256]{3,1,2,0:T(8,128)S(1)}, f32[8,16,8,256]{3,1,2,0:T(8,128)S(1)}, f32[8,4,8,256]{...) while((s32[]{:T(128)}, f32[8,4,8,128]{3,2,0,1:T(8,128)S(1)}, f32[8,16,8,256]{3,1,2,0:T(8,128)S(1)}, ...), condition=%wide.region_1.2_spmd, body=%wide.region_0.1_spmd.sunk | while | flops 222494848 | bytes 1852517 | solution.py:95
  50.2 25.9 %fusion.48 = f32[1,4,8,128]{3,1,2,0:T(4,128)S(1)} fusion(f32[16,8,256]{2,0,1:T(8,128)S(1)} %get-tuple-element.131, f32[16,8,256]{2,0,1:T(8,128)S(1)} %get-tuple-element.132, f32[16,8,256]{2,0,1:T(8,128)S(1)} %get-tuple-element.133, f32[16,8,256]{2,0,1:T(8,128)S(1)} %get-tuple-element.134, f32[128]{0:T(128)S(1)} %iota_convert_fusion.2, ...), kind=kOutput, calls=%fused_computation.14.clone.3 | convolution fusion | flops 222429184 | bytes 705024 | tf_op jit(solution)/shard_map/while/body/eval_jaxpr/bkri,krim->brm/dot_general | solution.py:93
  76.3 25.9 %fusion.48 = f32[1,4,8,128]{3,1,2,0:T(4,128)S(1)} fusion(f32[16,8,256]{2,0,1:T(8,128)S(1)} %get-tuple-element.131, f32[16,8,256]{2,0,1:T(8,128)S(1)} %get-tuple-element.132, f32[16,8,256]{2,0,1:T(8,128)S(1)} %get-tuple-element.133, f32[16,8,256]{2,0,1:T(8,128)S(1)} %get-tuple-element.134, f32[128]{0:T(128)S(1)} %iota_convert_fusion.2, ...), kind=kOutput, calls=%fused_computation.14.clone.3 | convolution fusion | flops 222429184 | bytes 705024 | tf_op jit(solution)/shard_map/while/body/eval_jaxpr/bkri,krim->brm/dot_general | solution.py:93
  102.3 25.9 %fusion.48 = f32[1,4,8,128]{3,1,2,0:T(4,128)S(1)} fusion(f32[16,8,256]{2,0,1:T(8,128)S(1)} %get-tuple-element.131, f32[16,8,256]{2,0,1:T(8,128)S(1)} %get-tuple-element.132, f32[16,8,256]{2,0,1:T(8,128)S(1)} %get-tuple-element.133, f32[16,8,256]{2,0,1:T(8,128)S(1)} %get-tuple-element.134, f32[128]{0:T(128)S(1)} %iota_convert_fusion.2, ...), kind=kOutput, calls=%fused_computation.14.clone.3 | convolution fusion | flops 222429184 | bytes 705024 | tf_op jit(solution)/shard_map/while/body/eval_jaxpr/bkri,krim->brm/dot_general | solution.py:93
  128.4 25.9 %fusion.48 = f32[1,4,8,128]{3,1,2,0:T(4,128)S(1)} fusion(f32[16,8,256]{2,0,1:T(8,128)S(1)} %get-tuple-element.131, f32[16,8,256]{2,0,1:T(8,128)S(1)} %get-tuple-element.132, f32[16,8,256]{2,0,1:T(8,128)S(1)} %get-tuple-element.133, f32[16,8,256]{2,0,1:T(8,128)S(1)} %get-tuple-element.134, f32[128]{0:T(128)S(1)} %iota_convert_fusion.2, ...), kind=kOutput, calls=%fused_computation.14.clone.3 | convolution fusion | flops 222429184 | bytes 705024 | tf_op jit(solution)/shard_map/while/body/eval_jaxpr/bkri,krim->brm/dot_general | solution.py:93
  154.4 25.9 %fusion.48 = f32[1,4,8,128]{3,1,2,0:T(4,128)S(1)} fusion(f32[16,8,256]{2,0,1:T(8,128)S(1)} %get-tuple-element.131, f32[16,8,256]{2,0,1:T(8,128)S(1)} %get-tuple-element.132, f32[16,8,256]{2,0,1:T(8,128)S(1)} %get-tuple-element.133, f32[16,8,256]{2,0,1:T(8,128)S(1)} %get-tuple-element.134, f32[128]{0:T(128)S(1)} %iota_convert_fusion.2, ...), kind=kOutput, calls=%fused_computation.14.clone.3 | convolution fusion | flops 222429184 | bytes 705024 | tf_op jit(solution)/shard_map/while/body/eval_jaxpr/bkri,krim->brm/dot_general | solution.py:93
  180.5 25.9 %fusion.48 = f32[1,4,8,128]{3,1,2,0:T(4,128)S(1)} fusion(f32[16,8,256]{2,0,1:T(8,128)S(1)} %get-tuple-element.131, f32[16,8,256]{2,0,1:T(8,128)S(1)} %get-tuple-element.132, f32[16,8,256]{2,0,1:T(8,128)S(1)} %get-tuple-element.133, f32[16,8,256]{2,0,1:T(8,128)S(1)} %get-tuple-element.134, f32[128]{0:T(128)S(1)} %iota_convert_fusion.2, ...), kind=kOutput, calls=%fused_computation.14.clone.3 | convolution fusion | flops 222429184 | bytes 705024 | tf_op jit(solution)/shard_map/while/body/eval_jaxpr/bkri,krim->brm/dot_general | solution.py:93
  206.5 25.9 %fusion.48 = f32[1,4,8,128]{3,1,2,0:T(4,128)S(1)} fusion(f32[16,8,256]{2,0,1:T(8,128)S(1)} %get-tuple-element.131, f32[16,8,256]{2,0,1:T(8,128)S(1)} %get-tuple-element.132, f32[16,8,256]{2,0,1:T(8,128)S(1)} %get-tuple-element.133, f32[16,8,256]{2,0,1:T(8,128)S(1)} %get-tuple-element.134, f32[128]{0:T(128)S(1)} %iota_convert_fusion.2, ...), kind=kOutput, calls=%fused_computation.14.clone.3 | convolution fusion | flops 222429184 | bytes 705024 | tf_op jit(solution)/shard_map/while/body/eval_jaxpr/bkri,krim->brm/dot_general | solution.py:93
  232.6 25.9 %fusion.48 = f32[1,4,8,128]{3,1,2,0:T(4,128)S(1)} fusion(f32[16,8,256]{2,0,1:T(8,128)S(1)} %get-tuple-element.131, f32[16,8,256]{2,0,1:T(8,128)S(1)} %get-tuple-element.132, f32[16,8,256]{2,0,1:T(8,128)S(1)} %get-tuple-element.133, f32[16,8,256]{2,0,1:T(8,128)S(1)} %get-tuple-element.134, f32[128]{0:T(128)S(1)} %iota_convert_fusion.2, ...), kind=kOutput, calls=%fused_computation.14.clone.3 | convolution fusion | flops 222429184 | bytes 705024 | tf_op jit(solution)/shard_map/while/body/eval_jaxpr/bkri,krim->brm/dot_general | solution.py:93
  259.3 2.7 broadcast_in_dim.93
  262.0 3.8 %all-to-all-start.2 = ((f32[16,1,37504]{2,1,0:T(1,128)}), f32[16,1,37504]{2,1,0:T(1,128)S(1)}, u32[]{:S(2)}, u32[]{:S(2)}) async-start(f32[16,1,37504]{2,1,0:T(1,128)} %broadcast_in_dim.93), calls=%async_computation.2 | async-start | bytes 4800512 | tf_op jit(solution)/shard_map/all_to_all | solution.py:18
  265.8 32.3 %all-to-all-done.2 = f32[16,1,37504]{2,1,0:T(1,128)S(1)} async-done(((f32[16,1,37504]{2,1,0:T(1,128)}), f32[16,1,37504]{2,1,0:T(1,128)S(1)}, u32[]{:S(2)}, u32[]{:S(2)}) %all-to-all-start.2) | async-done | bytes 2400288 | tf_op jit(solution)/shard_map/all_to_all | solution.py:18
  298.1 1.5 reduce_sum.57
  302.2 10.8 %all-to-all-start.3 = ((f32[16,1,4]{2,1,0:T(1,128)}), f32[16,1,4]{2,1,0:T(1,128)S(1)}, u32[]{:S(2)}, u32[]{:S(2)}) async-start(f32[16,1,4]{2,1,0:T(1,128)} %broadcast_in_dim.95), calls=%async_computation.3 | async-start | bytes 16384 | tf_op jit(solution)/shard_map/all_to_all | solution.py:18
  314.6 5.5 %all-to-all-done.3 = f32[16,1,4]{2,1,0:T(1,128)S(1)} async-done(((f32[16,1,4]{2,1,0:T(1,128)}), f32[16,1,4]{2,1,0:T(1,128)S(1)}, u32[]{:S(2)}, u32[]{:S(2)}) %all-to-all-start.3) | async-done | bytes 288 | tf_op jit(solution)/shard_map/all_to_all | solution.py:18
  (115 shorter events, 22.5 us)
Async XLA Ops:
  1.4 29.8 %collective-permute-start.1 = (f32[256]{0:T(256)S(1)}, f32[256]{0:T(256)S(1)}, u32[]{:S(2)}, u32[]{:S(2)}) collective-permute-start(f32[256]{0:T(256)S(1)} %bitcast.84), channel_id=1, source_target_pairs={{1,0},{2,1},{3,2},{4,3},{5,4},{6,5},{7,6},{8,7},{9,8},{10,9},{11,1... | collective-permute-start | bytes 3080 | tf_op jit(solution)/shard_map/ppermute | solution.py:44
  7.1 14.8 %all-to-all-start.1 = ((f32[16,1,256]{2,1,0:T(1,128)}), f32[16,1,256]{2,1,0:T(1,128)S(1)}, u32[]{:S(2)}, u32[]{:S(2)}) async-start(f32[16,1,256]{2,1,0:T(1,128)} %broadcast_in_dim.90), calls=%async_computation.1 | async-start | bytes 32768 | tf_op jit(solution)/shard_map/all_to_all | solution.py:18
  13.2 29.0 %collective-permute-start = (f32[16,256]{0,1:T(8,128)S(1)}, f32[16,256]{0,1:T(8,128)S(1)}, u32[]{:S(2)}, u32[]{:S(2)}) collective-permute-start(f32[16,256]{0,1:T(8,128)S(1)} %bitcast.76), channel_id=1, source_target_pairs={{1,0},{2,1},{3,2},{4,3},{5,4},{6,5},{7,6},{8,7},{9,8},{10,9},{11,1... | collective-permute-start | bytes 49160 | tf_op jit(solution)/shard_map/ppermute | solution.py:44
  16.7 14.4 %copy-start.5 = (s32[256]{0:T(256)S(1)}, s32[256]{0:T(256)}, u32[]{:S(2)}) copy-start(s32[256]{0:T(256)} %param.19) | copy-start | bytes 3076
  16.7 14.5 %copy-start.1 = (s32[64,256]{1,0:T(8,128)S(1)}, s32[64,256]{1,0:T(8,128)}, u32[]{:S(2)}) copy-start(s32[64,256]{1,0:T(8,128)} %param.17) | copy-start | bytes 196612
  22.6 19.8 %copy-start = (f32[16,64,256]{2,1,0:T(8,128)S(1)}, f32[16,64,256]{2,1,0:T(8,128)}, u32[]{:S(2)}) copy-start(f32[16,64,256]{2,1,0:T(8,128)} %param.12) | copy-start | bytes 3145732
  22.6 19.8 %copy-start.4 = (f32[64,256]{1,0:T(8,128)S(1)}, f32[64,256]{1,0:T(8,128)}, u32[]{:S(2)}) copy-start(f32[64,256]{1,0:T(8,128)} %param.14) | copy-start | bytes 196612
  22.6 15.3 %all-to-all-start = ((f32[16,16,256]{2,1,0:T(8,128)}), f32[16,16,256]{2,1,0:T(8,128)S(1)}, u32[]{:S(2)}, u32[]{:S(2)}) async-start(f32[16,16,256]{2,1,0:T(8,128)} %broadcast_in_dim.86), calls=%async_computation | async-start | bytes 524288 | tf_op jit(solution)/shard_map/all_to_all | solution.py:18
  42.4 2.4 copy-start.2
  48.8 1.2 copy-start.3
  262.0 36.1 %all-to-all-start.2 = ((f32[16,1,37504]{2,1,0:T(1,128)}), f32[16,1,37504]{2,1,0:T(1,128)S(1)}, u32[]{:S(2)}, u32[]{:S(2)}) async-start(f32[16,1,37504]{2,1,0:T(1,128)} %broadcast_in_dim.93), calls=%async_computation.2 | async-start | bytes 4800512 | tf_op jit(solution)/shard_map/all_to_all | solution.py:18
  302.2 17.9 %all-to-all-start.3 = ((f32[16,1,4]{2,1,0:T(1,128)}), f32[16,1,4]{2,1,0:T(1,128)S(1)}, u32[]{:S(2)}, u32[]{:S(2)}) async-start(f32[16,1,4]{2,1,0:T(1,128)} %broadcast_in_dim.95), calls=%async_computation.3 | async-start | bytes 16384 | tf_op jit(solution)/shard_map/all_to_all | solution.py:18
where the time goes:
time: 322 us
  matrix products  210 us (65%)
  waiting for transfers between devices  44.5 us (14%)
  starting transfers between devices  33.5 us (10%)
  local copies, waits for them, and re-layouts  20.7 us (6%)
  other arithmetic  11.5 us (4%)
    dot_general x8, matrix products, one_block(): jnp.einsum('bkri,krim->brm', weighted, tent, precision=lax.Precision.HIGH...  207 us
    all_to_all x4, waiting for transfers between devices, copy_for_each(): return lax.all_to_all(copies, axis, split_axis=0, concat_axis=0, tiled=True)  44.5 us
    all_to_all x4, starting transfers between devices, copy_for_each(): return lax.all_to_all(copies, axis, split_axis=0, concat_axis=0, tiled=True)  26.5 us
    ppermute x2, starting transfers between devices, passed_along(): return lax.ppermute(block, axis, route)  7.01 us
  transfers between devices with their start and end apart: 6, of which 3 were waited for; matrix products, arithmetic and copies ran while one was open for 5% of the time, Pallas kernels for 0%

commit v1 on v0

v1 whole, which is shorter than its diff:
```python
import math

import jax
import jax.numpy as jnp
from jax import lax
from jax.experimental import pallas as pl
from jax.experimental.pallas import tpu as pltpu
from jax.sharding import PartitionSpec as P

BINS = 128
REGIONS = 4
TIERS = 16
ROWS = 64
COLS = 256
NLON = 16
NLAT = 16
GROUP = 8
OWNED = ROWS // NLON
HI = 16
LO = BINS // HI
PAY = 24

HEAT, THETA, WET, FLUX, SOUTH = 64, 68, 69, 72, 76

UNIT = math.sqrt(BINS / (COLS * NLON * TIERS))
IMPLIED = 2.0 / math.sqrt(COLS * NLON * ROWS * NLAT)
F32, BF16 = jnp.float32, jnp.bfloat16


def iota(shape, dim):
    return lax.broadcasted_iota(jnp.int32, shape, dim)


def two_terms(x):
    high = x.astype(BF16).astype(F32)
    return high, x - high


def kernel(
    speed_h, theta_h, dz_s, dx_h, area_h, flux_h, tally_h, region_h, seam_s,
    out_class, out_over, out_heat, out_impl,
    th, sp, dx, area, flux, tally, region, bc, part, crow, sfin,
    rs_send, rs_recv, ag_send, ag_recv,
    halo_send, halo_recv, fold_send, fold_recv, pfx_send, pfx_recv,
    in_sem, rs_ssem, rs_rsem, ag_ssem, ag_rsem, fold_ssem, fold_rsem,
    halo_ssem, halo_rsem, pfx_ssem, pfx_rsem,
):
    o = lax.axis_index("lon")
    l = lax.axis_index("lat")
    lane8 = iota((8, 128), 1)

    loads = [
        pltpu.make_async_copy(flux_h, flux, in_sem.at[0]),
        pltpu.make_async_copy(area_h, area, in_sem.at[1]),
        pltpu.make_async_copy(region_h, region, in_sem.at[2]),
        pltpu.make_async_copy(tally_h, tally.at[pl.ds(0, ROWS)], in_sem.at[3]),
        pltpu.make_async_copy(dx_h, dx, in_sem.at[4]),
        pltpu.make_async_copy(theta_h, th.at[:, pl.ds(0, ROWS)], in_sem.at[5]),
        pltpu.make_async_copy(speed_h, sp, in_sem.at[6]),
    ]
    for load in loads:
        load.start()

    barrier = pltpu.get_barrier_semaphore()
    for d in range(1, NLON):
        pl.semaphore_signal(barrier, inc=1, device_id={"lon": lax.rem(o + d, NLON)}, device_id_type=pl.DeviceIdType.MESH)
    for d in range(1, NLAT):
        pl.semaphore_signal(barrier, inc=1, device_id={"lat": lax.rem(l + d, NLAT)}, device_id_type=pl.DeviceIdType.MESH)
    for load in loads:
        load.wait()

    acc = [jnp.zeros((8, COLS), F32) for _ in range(REGIONS)]
    for g in range(ROWS // 8):
        rows = slice(8 * g, 8 * g + 8)
        f = flux[rows, :] * area[rows, :]
        reg = region[rows, :]
        for b in range(REGIONS):
            acc[b] = acc[b] + jnp.where(reg == b, f, 0.0)
    totals = jnp.zeros((8, 128), F32)
    for b in range(REGIONS):
        t = jnp.sum(jnp.sum(acc[b], axis=0, keepdims=True), axis=1, keepdims=True)
        totals = jnp.where(lane8 == SOUTH + b, t, totals)
    pfx_send[...] = totals

    for k in range(TIERS):
        halo_send[k : k + 1, :] = th[k, 0:1, :]
        fold_send[k : k + 1, :] = th[k, ROWS - 1 : ROWS, :]
    halo_send[TIERS:24, :] = jnp.broadcast_to(tally[0:1, :].astype(F32), (8, COLS))
    fold_send[TIERS:24, :] = jnp.broadcast_to(tally[ROWS - 1 : ROWS, :].astype(F32), (8, COLS))

    def halo_copy():
        return pltpu.make_async_remote_copy(
            halo_send, halo_recv, halo_ssem, halo_rsem, device_id={"lat": lax.max(l - 1, 0)},
            device_id_type=pl.DeviceIdType.MESH)

    def fold_copy(dst, src):
        return pltpu.make_async_remote_copy(
            fold_send, fold_recv.at[src], fold_ssem.at[dst], fold_rsem.at[src],
            device_id={"lon": dst}, device_id_type=pl.DeviceIdType.MESH)

    def pfx_copy(dst, src):
        return pltpu.make_async_remote_copy(
            pfx_send, pfx_recv.at[src], pfx_ssem.at[dst], pfx_rsem.at[src],
            device_id={"lat": dst}, device_id_type=pl.DeviceIdType.MESH)

    def rs_copy(dst, src):
        return pltpu.make_async_remote_copy(
            rs_send.at[dst], rs_recv.at[src], rs_ssem.at[dst], rs_rsem.at[src],
            device_id={"lon": dst}, device_id_type=pl.DeviceIdType.MESH)

    def ag_copy(dst, src):
        return pltpu.make_async_remote_copy(
            ag_send, ag_recv.at[src], ag_ssem.at[dst], ag_rsem.at[src],
            device_id={"lon": dst}, device_id_type=pl.DeviceIdType.MESH)

    def others(count, me, act):
        def step(q, c):
            @pl.when(q != me)
            def _():
                act(q)
            return c
        lax.fori_loop(0, count, step, 0)

    def first_sends():
        pl.semaphore_wait(barrier, NLON - 1 + NLAT - 1)

        @pl.when(l > 0)
        def _():
            halo_copy().start()

        @pl.when(l == NLAT - 1)
        def _():
            others(NLON, o, lambda q: fold_copy(q, o).start())
            fold_recv[o] = fold_send[...]

        def north(q, c):
            @pl.when(q > l)
            def _():
                pfx_copy(q, l).start()
            return c
        lax.fori_loop(0, NLAT, north, 0)

    def north_row():
        @pl.when(l < NLAT - 1)
        def _():
            halo_copy().wait_recv()
            for k in range(TIERS):
                th[k, ROWS : ROWS + 1, :] = halo_recv[k : k + 1, :]
            tally[ROWS : ROWS + 1, :] = halo_recv[TIERS : TIERS + 1, :].astype(jnp.int32)

        @pl.when(l == NLAT - 1)
        def _():
            others(NLON, o, lambda q: fold_copy(o, q).wait_recv())
            first = seam_s[0]
            owner = lax.shift_right_logical(first, 8)
            at = jnp.bitwise_and(first, COLS - 1)
            high = fold_recv[owner]
            low = fold_recv[jnp.bitwise_and(owner + NLON - 1, NLON - 1)]
            for t in range(COLS // 128):
                i = lane8 + 128 * t
                spot = jnp.bitwise_and(at - i, COLS - 1)
                lane = jnp.bitwise_and(spot, 127)
                for r in range(3):
                    rows = slice(8 * r, 8 * r + 8)
                    pick = [
                        jnp.where(
                            spot >= 128,
                            jnp.take_along_axis(src[rows, 128:], lane, axis=1),
                            jnp.take_along_axis(src[rows, :128], lane, axis=1),
                        )
                        for src in (high, low)
                    ]
                    halo_recv[rows, 128 * t : 128 * t + 128] = jnp.where(i <= at, pick[0], pick[1])
            for k in range(TIERS):
                th[k, ROWS : ROWS + 1, :] = halo_recv[k : k + 1, :]
            tally[ROWS : ROWS + 1, :] = halo_recv[TIERS : TIERS + 1, :].astype(jnp.int32)

        def south(q, c):
            @pl.when(q < l)
            def _():
                pfx_copy(l, q).wait_recv()
            return c
        lax.fori_loop(0, NLAT, south, 0)

    sub8 = iota((8, COLS), 0)
    hi_iota = iota((HI, COLS), 0).astype(F32).astype(BF16)
    cl_iota = iota((REGIONS * LO, COLS), 0).astype(F32).astype(BF16)
    zero16 = jnp.zeros((HI, COLS), BF16)
    one32 = jnp.ones((REGIONS * LO, COLS), BF16)
    zero32 = jnp.zeros((REGIONS * LO, COLS), BF16)

    def group(g, carry):
        @pl.when(g == ROWS // GROUP - 1)
        def _():
            north_row()

        base = pl.multiple_of(g * GROUP, GROUP)
        here = pl.ds(base, GROUP)
        nxt = pl.ds(base + GROUP, 1)
        deep = tally[here, :]
        deep_n = jnp.where(sub8 == 7, tally[nxt, :], pltpu.roll(deep, 7, 0))
        face_depth = jnp.minimum(deep, deep_n)
        width = dx[here, :]
        reg = region[here, :]
        regf = reg.astype(F32)
        member = [reg == b for b in range(REGIONS)]
        heat = jnp.zeros((8, COLS), F32)
        theta_sum = jnp.zeros((8, COLS), F32)
        wet_sum = jnp.zeros((8, COLS), F32)
        stats = jnp.zeros((8, 128), F32)
        for k in range(TIERS):
            t = th[k, here, :]
            tn = jnp.where(sub8 == 7, th[k, nxt, :], pltpu.roll(t, 7, 0))
            face = 0.5 * (t + tn)
            vol = jnp.where(face_depth > k, dz_s[k] * width, 0.0)
            mass = vol * sp[k, here, :]
            pos = jnp.clip((face - (-2.0)) * (BINS / 32.0), 0.0, BINS - 1.0)
            low = jnp.minimum(jnp.floor(pos), BINS - 2.0)
            w = pos - low
            hi = jnp.floor(low * (1.0 / LO))
            bc[0, k] = hi
            bc[1, k] = (low - hi * LO) + regf * LO
            s0, s1 = two_terms(mass)
            bc[2, k] = s0
            bc[3, k] = s1
            s0, s1 = two_terms(mass * w)
            bc[4, k] = s0
            bc[5, k] = s1
            heat = heat + mass * face
            theta_sum = theta_sum + vol * face
            wet_sum = wet_sum + vol
            for b in range(REGIONS):
                red = jnp.sum(jnp.where(member[b], mass, 0.0), axis=1, keepdims=True)
                stats = jnp.where(lane8 == b * TIERS + k, red, stats)
        f = flux[here, :] * area[here, :]
        for b in range(REGIONS):
            red = jnp.sum(jnp.where(member[b], heat, 0.0), axis=1, keepdims=True)
            stats = jnp.where(lane8 == HEAT + b, red, stats)
            red = jnp.sum(jnp.where(member[b], f, 0.0), axis=1, keepdims=True)
            stats = jnp.where(lane8 == FLUX + b, red, stats)
        stats = jnp.where(lane8 == THETA, jnp.sum(theta_sum, axis=1, keepdims=True), stats)
        stats = jnp.where(lane8 == WET, jnp.sum(wet_sum, axis=1, keepdims=True), stats)
        for h in range(2):
            rs_send[2 * g + h, 16:20, :] = stats[4 * h : 4 * h + 4, :]

        @pl.when(g == ROWS // GROUP - 1)
        def _():
            def add(q, c):
                return c + jnp.where(q < l, pfx_recv[q], 0.0)
            south = lax.fori_loop(0, NLAT, add, jnp.zeros((8, 128), F32))
            rs_send[2 * g + 1, 16:24, :] = rs_send[2 * g + 1, 16:24, :] + south

        for jj in range(GROUP):
            total = None
            for k in range(TIERS):
                def row(n, rows):
                    return jnp.broadcast_to(bc[n, k, jj : jj + 1, :], (rows, COLS)).astype(BF16)
                mask = row(0, HI) == hi_iota
                lhs = jnp.concatenate(
                    [jnp.where(mask, row(n, HI), zero16) for n in (2, 3, 4, 5)], axis=0)
                rhs = jnp.where(row(1, REGIONS * LO) == cl_iota, one32, zero32)
                d = lax.dot_general(lhs, rhs, (((1,), (1,)), ((), ())), preferred_element_type=F32)
                total = d if total is None else total + d
            lanes = slice(32 * (jj % 4), 32 * (jj % 4) + 32)
            part[jj // 4, 0:HI, lanes] = total[0:HI] + total[HI : 2 * HI]
            part[jj // 4, HI : 2 * HI, lanes] = total[2 * HI : 3 * HI] + total[3 * HI :]
        lane16 = iota((HI, 128), 1)
        first_hi = iota((HI, 128), 0) == 0
        for h in range(2):
            s0 = part[h, 0:HI, :]
            s1 = part[h, HI : 2 * HI, :]
            up = jnp.where(first_hi, 0.0, pltpu.roll(pltpu.roll(s1, 128 - (LO - 1), 1), 1, 0))
            moved = jnp.where(jnp.bitwise_and(lane16, LO - 1) == 0, up, pltpu.roll(s1, 1, 1))
            rs_send[2 * g + h, 0:HI, :] = s0 - s1 + moved

        @pl.when(g == 0)
        def _():
            first_sends()

        for h in range(2):
            @pl.when(2 * g + h != o)
            def _():
                rs_copy(2 * g + h, o).start()
        return carry

    lax.fori_loop(0, ROWS // GROUP, group, 0)

    others(NLON, o, lambda q: rs_copy(o, q).wait_recv())

    def add(q, c):
        return c + jnp.where(q != o, rs_recv[q], 0.0)

    own = lax.fori_loop(0, NLON, add, rs_send[o])
    crow[...] = own[0:HI]
    sub = iota((8, 128), 0)
    block = lax.shift_right_logical(lane8, 3)
    for v in range(2):
        r = sub + 8 * v
        index = 32 * jnp.bitwise_and(r, 3) + 8 * lax.shift_right_logical(r, 2) + jnp.bitwise_and(lane8, LO - 1)
        res = jnp.zeros((8, 128), F32)
        for hi in range(HI):
            spread = jnp.broadcast_to(crow[hi : hi + 1, :], (8, 128))
            res = jnp.where(block == hi, jnp.take_along_axis(spread, index, axis=1), res)
        ag_send[8 * v : 8 * v + 8, :] = res
    ag_send[16:24, :] = own[16:24]
    others(NLON, o, lambda q: ag_copy(q, o).start())
    ag_recv[o] = ag_send[...]
    others(NLON, o, lambda q: ag_copy(o, q).wait_recv())

    for s in range(NLON):
        for b in range(REGIONS):
            out_class[b, 4 * s : 4 * s + 4, :] = UNIT * ag_recv[s, 4 * b : 4 * b + 4, :]
        sfin[4 * s : 4 * s + 4, :] = ag_recv[s, 16:20, :]
    sfin[ROWS:128, :] = jnp.zeros((128 - ROWS, 128), F32)
    rowsum = sfin[0:ROWS, :]
    lanes = iota((ROWS, 128), 1)
    x = rowsum
    for step in (1, 2, 4, 8):
        x = x + jnp.where(jnp.bitwise_and(lanes, 15) >= step, pltpu.roll(x, step, 1), 0.0)
    for b in range(REGIONS):
        out_over[b] = UNIT * x[:, 16 * b : 16 * b + 16]
    flipped = jnp.transpose(sfin[...])
    wet = flipped[WET : WET + 1, :]
    mean = flipped[THETA : THETA + 1, :] / jnp.where(iota((1, 128), 1) < ROWS, wet, 1.0)
    for b in range(REGIONS):
        vol = jnp.sum(flipped[16 * b : 16 * b + 16, :], axis=0, keepdims=True)
        res = (UNIT / 16.0) * (flipped[HEAT + b : HEAT + b + 1, :] - vol * mean)
        out_heat[b : b + 1, :] = res[:, 0:ROWS]
    c = flipped[FLUX : FLUX + 8, :]
    south = jnp.sum(jnp.where(lane8 == ROWS - 1, c, 0.0), axis=1, keepdims=True)
    for step in (1, 2, 4, 8, 16, 32):
        c = c + jnp.where(lane8 >= step, pltpu.roll(c, step, 1), 0.0)
    out_impl[...] = (IMPLIED * (c[0:4] + south[4:8]))[:, 0:ROWS]

    others(NLON, o, lambda q: rs_copy(q, o).wait_send())
    others(NLON, o, lambda q: ag_copy(q, o).wait_send())

    @pl.when(l > 0)
    def _():
        halo_copy().wait_send()

    @pl.when(l == NLAT - 1)
    def _():
        others(NLON, o, lambda q: fold_copy(q, o).wait_send())

    def north_done(q, c):
        @pl.when(q > l)
        def _():
            pfx_copy(q, l).wait_send()
        return c
    lax.fori_loop(0, NLAT, north_done, 0)


def body(speed, theta, dz, dx, area, flux, tally, region, seam):
    any_ = pl.BlockSpec(memory_space=pl.ANY)
    smem = pl.BlockSpec(memory_space=pltpu.SMEM)
    vmem = pl.BlockSpec(memory_space=pltpu.VMEM)
    dma = pltpu.SemaphoreType.DMA
    return pl.pallas_call(
        kernel,
        out_shape=(
            jax.ShapeDtypeStruct((REGIONS, ROWS, BINS), F32),
            jax.ShapeDtypeStruct((REGIONS, ROWS, TIERS), F32),
            jax.ShapeDtypeStruct((REGIONS, ROWS), F32),
            jax.ShapeDtypeStruct((REGIONS, ROWS), F32),
        ),
        in_specs=[any_, any_, smem, any_, any_, any_, any_, any_, smem],
        out_specs=(vmem, vmem, vmem, vmem),
        scratch_shapes=[
            pltpu.VMEM((TIERS, ROWS + 8, COLS), F32),
            pltpu.VMEM((TIERS, ROWS, COLS), F32),
            pltpu.VMEM((ROWS, COLS), F32),
            pltpu.VMEM((ROWS, COLS), F32),
            pltpu.VMEM((ROWS, COLS), F32),
            pltpu.VMEM((ROWS + 8, COLS), jnp.int32),
            pltpu.VMEM((ROWS, COLS), jnp.int32),
            pltpu.VMEM((6, TIERS, GROUP, COLS), F32),
            pltpu.VMEM((2, 2 * HI, 128), F32),
            pltpu.VMEM((HI, 128), F32),
            pltpu.VMEM((128, 128), F32),
            pltpu.VMEM((NLON, PAY, 128), F32),
            pltpu.VMEM((NLON, PAY, 128), F32),
            pltpu.VMEM((PAY, 128), F32),
            pltpu.VMEM((NLON, PAY, 128), F32),
            pltpu.VMEM((24, COLS), F32),
            pltpu.VMEM((24, COLS), F32),
            pltpu.VMEM((24, COLS), F32),
            pltpu.VMEM((NLON, 24, COLS), F32),
            pltpu.VMEM((8, 128), F32),
            pltpu.VMEM((NLAT, 8, 128), F32),
            dma((7,)),
            dma((NLON,)), dma((NLON,)), dma((NLON,)), dma((NLON,)), dma((NLON,)), dma((NLON,)),
            dma, dma,
            dma((NLAT,)), dma((NLAT,)),
        ],
        compiler_params=pltpu.CompilerParams(collective_id=0, has_side_effects=True),
    )(speed, theta, dz, dx, area, flux, tally, region, seam)


def solution(mesh):
    in_specs = (
        P(None, "lat", "lon"),
        P(None, "lat", "lon"),
        P(),
        P("lat", "lon"),
        P("lat", "lon"),
        P("lat", "lon"),
        P("lat", "lon"),
        P("lat", "lon"),
        P("lon"),
    )
    out_specs = (P(None, "lat", None), P(None, "lat", None), P(None, "lat"), P(None, "lat"))
    return jax.shard_map(body, mesh=mesh, in_specs=in_specs, out_specs=out_specs, check_vma=False)
```

time: 322 us -> 42.4 us (0.13)
  matrix products: 210 us -> 0 us
  waiting for transfers between devices: 44.5 us -> 0 us
  Pallas kernels: 0 us -> 38 us
  starting transfers between devices: 33.5 us -> 0 us
  local copies, waits for them, and re-layouts: 20.7 us -> 3.57 us
  other arithmetic: 11.5 us -> 0 us
    dot_general x11 -> x0, matrix products: 210 us -> none  [the longest x8 207 us: one_block(): jnp.einsum('bkri,krim->brm', weighted, tent, precision=lax.Precision.HIGH...]
    all_to_all x4 -> x0, waiting for transfers between devices: 44.5 us -> none  [copy_for_each(): return lax.all_to_all(copies, axis, split_axis=0, concat_axis=0, tiled=True)]
    pallas_call x0 -> x1, Pallas kernels: none -> 38 us  [body(): pl.pallas_call(kernel, out_shape=(jax.ShapeDtypeStruct((REGIONS, ROWS, BI...]
    all_to_all x4 -> x0, starting transfers between devices: 26.5 us -> none  [copy_for_each(): return lax.all_to_all(copies, axis, split_axis=0, concat_axis=0, tiled=True)]
    ppermute x2 -> x0, starting transfers between devices: 7.01 us -> none  [passed_along(): return lax.ppermute(block, axis, route)]
    broadcast_in_dim x5 -> x0, local copies, waits for them, and re-layouts: 4.67 us -> none  [the longest x4 4.61 us: copy_for_each(): copies = jnp.broadcast_to(array, (lax.axis_size(axis), *array.shape))]
    reduce_sum x4 -> x0, other arithmetic: 4.18 us -> none  [the longest x1 2.43 us: vertical_aggregate_field(): jnp.sum(water_capacity * interface_theta, axis=(0, 2))]
    gather x2 -> x0, local copies, waits for them, and re-layouts: 4.03 us -> none  [the longest x1 2.31 us: body(): reflected_theta = jnp.take(seam_theta, seam_matching_meridian, axis=1)]
  transfers between devices with their start and end apart: 6 -> 0, of which waited for: 3 -> 0; matrix products, arithmetic and copies ran while one was open for 5% -> 0% of each run, Pallas kernels for 0% -> 0%
where the time goes in v1:
time: 42.4 us; the launch traced here: 42.2 us
  Pallas kernels  38 us (90%)
  local copies, waits for them, and re-layouts  3.57 us (8%)
  between operations  0.65 us (2%)
    pallas_call x1, Pallas kernels, body(): pl.pallas_call(kernel, out_shape=(jax.ShapeDtypeStruct((REGIONS, ROWS, BI...  38 us
    unnamed x9, local copies, waits for them, and re-layouts  1.93 us
    pallas_call x1, local copies, waits for them, and re-layouts, body(): pl.pallas_call(kernel, out_shape=(jax.ShapeDtypeStruct((REGIONS, ROWS, BI...  1.64 us

profile of v1, /device:TPU:1, one launch (start us, length us, event | category | flops | bytes accessed | tf_op | source)
XLA Modules:
  0.0 42.2 jit_solution(2659175934630354150)
XLA Ops:
  0.6 38.0 %shard_map.120 = (f32[4,64,128]{2,1,0:T(8,128)}, f32[4,64,16]{2,1,0:T(8,128)}, f32[4,64]{1,0:T(4,128)}, f32[4,64]{1,0:T(4,128)}) custom-call(f32[16,64,256]{2,1,0:T(8,128)} %speed_h.1, f32[16,64,256]{2,1,0:T(8,128)} %theta_h.1, f32[16]{0:T(128)} %dz_s.1, f32[64,256]{1,0:T(8,128)} %dx_h.1, f32[64,256]{1,0:T(8,128)} %area_h.1, f32[64,256]{1,0:T(8,128)} %flux_h.1, ...), custom_call_target="tpu_custom_call" | custom-call | tf_op jit(solution)/shard_map/pallas_call | solution.py:359
  38.7 0.0 copy-start
  38.7 1.6 %copy.13 = f32[4,64,16]{1,2,0:T(8,128)} copy(f32[4,64,16]{2,1,0:T(8,128)} %get-tuple-element.5) | data formatting | bytes 32768 | tf_op jit(solution)/shard_map/pallas_call | solution.py:359
  40.3 0.0 copy-done
  40.3 0.0 copy-start.2
  40.3 0.7 %copy.17 = f32[4,64,128]{2,1,0:T(8,128)} copy(f32[4,64,128]{2,1,0:T(8,128)S(1)} %copy-done) | data formatting | bytes 262144
  41.0 0.0 copy-done.2
  41.0 0.0 copy-start.1
  41.0 0.6 %copy.18 = f32[4,64]{1,0:T(4,128)} copy(f32[4,64]{1,0:T(4,128)S(1)} %copy-done.2) | data formatting | bytes 2048
  41.6 0.1 copy-done.1
  41.7 0.6 %copy.19 = f32[4,64]{1,0:T(4,128)} copy(f32[4,64]{1,0:T(4,128)S(1)} %copy-done.1) | data formatting | bytes 2048
Async XLA Ops:
  38.7 1.7 %copy-start = (f32[4,64,128]{2,1,0:T(8,128)S(1)}, f32[4,64,128]{2,1,0:T(8,128)}, u32[]{:S(2)}) copy-start(f32[4,64,128]{2,1,0:T(8,128)} %get-tuple-element.12) | copy-start | bytes 393220
  40.3 0.7 %copy-start.2 = (f32[4,64]{1,0:T(4,128)S(1)}, f32[4,64]{1,0:T(4,128)}, u32[]{:S(2)}) copy-start(f32[4,64]{1,0:T(4,128)} %get-tuple-element.14) | copy-start | bytes 3076
  41.0 0.7 %copy-start.1 = (f32[4,64]{1,0:T(4,128)S(1)}, f32[4,64]{1,0:T(4,128)}, u32[]{:S(2)}) copy-start(f32[4,64]{1,0:T(4,128)} %get-tuple-element.15) | copy-start | bytes 3076

commit v2 on v1

v2 whole, which is shorter than its diff:
```python
import math

import jax
import jax.numpy as jnp
from jax import lax
from jax.experimental import pallas as pl
from jax.experimental.pallas import tpu as pltpu
from jax.sharding import PartitionSpec as P

BINS = 128
REGIONS = 4
TIERS = 16
ROWS = 64
COLS = 256
NLON = 16
NLAT = 16
GROUP = 8
OWNED = ROWS // NLON
LO = 12
HI = 11
SIDE = REGIONS * LO

HEAT, THETA, WET, FLUX, SOUTH = 64, 68, 69, 72, 76

UNIT = math.sqrt(BINS / (COLS * NLON * TIERS))
IMPLIED = 2.0 / math.sqrt(COLS * NLON * ROWS * NLAT)
VMEM_LIMIT = 66_800_000
F32, BF16 = jnp.float32, jnp.bfloat16


def iota(shape, dim):
    return lax.broadcasted_iota(jnp.int32, shape, dim)


def two_terms(x):
    high = x.astype(BF16).astype(F32)
    return high, x - high


def kernel(
    speed_h, theta_h, dz_s, dx_h, area_h, flux_h, tally_h, region_h, seam_s,
    out_class, out_sums,
    th, sp, dx, area, flux, tally, region,
    hi_a, cl_a, val_a, part_a, hi_b, cl_b, val_b, part_b,
    rs_send, rs_recv, ag_send,
    halo_send, halo_recv, fold_send, fold_recv, pfx_send, pfx_recv,
    in_sem, rs_ssem, rs_rsem, ag_ssem, agc_rsem, ags_rsem, fold_ssem, fold_rsem,
    halo_ssem, halo_rsem, pfx_ssem, pfx_rsem,
):
    o = lax.axis_index("lon")
    l = lax.axis_index("lat")
    lane8 = iota((8, 128), 1)
    MESH = pl.DeviceIdType.MESH

    first, rest = pl.ds(0, 16), pl.ds(16, ROWS - 16)
    loads = [
        pltpu.make_async_copy(flux_h, flux, in_sem.at[0]),
        pltpu.make_async_copy(area_h, area, in_sem.at[1]),
        pltpu.make_async_copy(region_h, region, in_sem.at[2]),
        pltpu.make_async_copy(tally_h, tally.at[pl.ds(0, ROWS)], in_sem.at[3]),
        pltpu.make_async_copy(dx_h, dx, in_sem.at[4]),
        pltpu.make_async_copy(theta_h.at[:, first], th.at[:, first], in_sem.at[5]),
        pltpu.make_async_copy(speed_h.at[:, first], sp.at[:, first], in_sem.at[6]),
        pltpu.make_async_copy(theta_h.at[:, rest], th.at[:, rest], in_sem.at[7]),
        pltpu.make_async_copy(speed_h.at[:, rest], sp.at[:, rest], in_sem.at[8]),
    ]
    for load in loads:
        load.start()

    barrier = pltpu.get_barrier_semaphore()
    for d in range(1, NLON):
        pl.semaphore_signal(barrier, inc=1, device_id={"lon": lax.rem(o + d, NLON)}, device_id_type=MESH)
    for d in range(1, NLAT):
        pl.semaphore_signal(barrier, inc=1, device_id={"lat": lax.rem(l + d, NLAT)}, device_id_type=MESH)

    def halo_copy():
        return pltpu.make_async_remote_copy(
            halo_send, halo_recv, halo_ssem, halo_rsem, device_id={"lat": lax.max(l - 1, 0)}, device_id_type=MESH)

    def fold_copy(dst, src):
        return pltpu.make_async_remote_copy(
            fold_send, fold_recv.at[src], fold_ssem.at[dst], fold_rsem.at[src],
            device_id={"lon": dst}, device_id_type=MESH)

    def pfx_copy(dst, src):
        return pltpu.make_async_remote_copy(
            pfx_send, pfx_recv.at[src], pfx_ssem.at[dst], pfx_rsem.at[src],
            device_id={"lat": dst}, device_id_type=MESH)

    def owner(g, t):
        if t < REGIONS:
            return 4 * t + lax.rem(g, 4), lax.div(g, 4)
        return 4 * lax.div(g, 2) + lax.rem(g + 1, 4), 2

    def rs_copy(g, t, src):
        dst, slot = owner(g, t)
        return pltpu.make_async_remote_copy(
            rs_send.at[g, t], rs_recv.at[slot, src], rs_ssem.at[g, t], rs_rsem.at[slot, src],
            device_id={"lon": dst}, device_id_type=MESH)

    def class_copy(slot, b, g, dst):
        return pltpu.make_async_remote_copy(
            ag_send.at[slot], out_class.at[b, pl.ds(pl.multiple_of(8 * g, 8), 8)],
            ag_ssem.at[slot, dst], agc_rsem.at[b, g], device_id={"lon": dst}, device_id_type=MESH)

    def sums_copy(g, dst):
        return pltpu.make_async_remote_copy(
            ag_send.at[2], out_sums.at[pl.ds(pl.multiple_of(8 * g, 8), 8)],
            ag_ssem.at[2, dst], ags_rsem.at[g], device_id={"lon": dst}, device_id_type=MESH)

    def others(count, me, act):
        def step(q, c):
            @pl.when(q != me)
            def _():
                act(q)
            return c
        lax.fori_loop(0, count, step, 0)

    def flux_totals():
        acc = [jnp.zeros((8, COLS), F32) for _ in range(REGIONS)]
        for g in range(ROWS // 8):
            rows = slice(8 * g, 8 * g + 8)
            f = flux[rows, :] * area[rows, :]
            reg = region[rows, :]
            for b in range(REGIONS):
                acc[b] = acc[b] + jnp.where(reg == b, f, 0.0)
        totals = jnp.zeros((8, 128), F32)
        for b in range(REGIONS):
            t = jnp.sum(jnp.sum(acc[b], axis=0, keepdims=True), axis=1, keepdims=True)
            totals = jnp.where(lane8 == SOUTH + b, t, totals)
        pfx_send[...] = totals

    def edge_rows():
        for k in range(TIERS):
            halo_send[k : k + 1, :] = th[k, 0:1, :]
            fold_send[k : k + 1, :] = th[k, ROWS - 1 : ROWS, :]
        halo_send[TIERS:24, :] = jnp.broadcast_to(tally[0:1, :].astype(F32), (8, COLS))
        fold_send[TIERS:24, :] = jnp.broadcast_to(tally[ROWS - 1 : ROWS, :].astype(F32), (8, COLS))

    def first_sends():
        pl.semaphore_wait(barrier, NLON - 1 + NLAT - 1)

        @pl.when(l == NLAT - 1)
        def _():
            others(NLON, o, lambda q: fold_copy(q, o).start())
            fold_recv[o] = fold_send[...]

        @pl.when(l > 0)
        def _():
            halo_copy().start()

        def north(q, c):
            @pl.when(q > l)
            def _():
                pfx_copy(q, l).start()
            return c
        lax.fori_loop(0, NLAT, north, 0)

    def north_row():
        @pl.when(l < NLAT - 1)
        def _():
            halo_copy().wait_recv()

        @pl.when(l == NLAT - 1)
        def _():
            others(NLON, o, lambda q: fold_copy(o, q).wait_recv())
            first = seam_s[0]
            source = lax.shift_right_logical(first, 8)
            at = jnp.bitwise_and(first, COLS - 1)
            high = fold_recv[source]
            low = fold_recv[jnp.bitwise_and(source + NLON - 1, NLON - 1)]
            for t in range(COLS // 128):
                i = lane8 + 128 * t
                spot = jnp.bitwise_and(at - i, COLS - 1)
                lane = jnp.bitwise_and(spot, 127)
                for r in range(3):
                    rows = slice(8 * r, 8 * r + 8)
                    pick = [
                        jnp.where(
                            spot >= 128,
                            jnp.take_along_axis(src[rows, 128:], lane, axis=1),
                            jnp.take_along_axis(src[rows, :128], lane, axis=1),
                        )
                        for src in (high, low)
                    ]
                    halo_recv[rows, 128 * t : 128 * t + 128] = jnp.where(i <= at, pick[0], pick[1])

        for k in range(TIERS):
            th[k, ROWS : ROWS + 1, :] = halo_recv[k : k + 1, :]
        tally[ROWS : ROWS + 1, :] = halo_recv[TIERS : TIERS + 1, :].astype(jnp.int32)

        def south(q, c):
            @pl.when(q < l)
            def _():
                pfx_copy(l, q).wait_recv()
            return c
        lax.fori_loop(0, NLAT, south, 0)

    sub8 = iota((8, COLS), 0)
    hi_iota = lax.shift_right_logical(iota((SIDE, COLS), 0), 2).astype(F32).astype(BF16)
    cl_iota = iota((SIDE, COLS), 0).astype(F32).astype(BF16)
    zero = jnp.zeros((SIDE, COLS), BF16)
    one = jnp.ones((SIDE, COLS), BF16)

    def prepare(g, hi_r, cl_r, val_r, south=None):
        base = g * GROUP if isinstance(g, int) else pl.multiple_of(g * GROUP, GROUP)
        here = pl.ds(base, GROUP)
        nxt = pl.ds(base + GROUP, 1)
        deep = tally[here, :]
        face_depth = jnp.minimum(deep, jnp.where(sub8 == 7, tally[nxt, :], pltpu.roll(deep, 7, 0)))
        width = dx[here, :]
        reg = region[here, :]
        regf = reg.astype(F32) * LO
        member = [reg == b for b in range(REGIONS)]
        heat = theta_sum = wet_sum = jnp.zeros((8, COLS), F32)
        stats = jnp.zeros((8, 128), F32)
        for k in range(TIERS):
            t = th[k, here, :]
            face = 0.5 * (t + jnp.where(sub8 == 7, th[k, nxt, :], pltpu.roll(t, 7, 0)))
            vol = jnp.where(face_depth > k, dz_s[k] * width, 0.0)
            mass = vol * sp[k, here, :]
            pos = jnp.clip((face - (-2.0)) * (BINS / 32.0), 0.0, BINS - 1.0)
            low = jnp.minimum(jnp.floor(pos), BINS - 2.0)
            hi = jnp.floor((low + 0.5) * (1.0 / LO))
            hi_r[k] = hi
            cl_r[k] = (low - hi * LO) + regf
            for n, x in enumerate(two_terms(mass) + two_terms(mass * (pos - low))):
                for half in range(2):
                    val_r[k, half, pl.ds(n, 8, stride=8), :] = x[:, 128 * half : 128 * half + 128]
                    val_r[k, half, pl.ds(n + 4, 8, stride=8), :] = x[:, 128 * half : 128 * half + 128]
            heat = heat + mass * face
            theta_sum = theta_sum + vol * face
            wet_sum = wet_sum + vol
            for b in range(REGIONS):
                red = jnp.sum(jnp.where(member[b], mass, 0.0), axis=1, keepdims=True)
                stats = jnp.where(lane8 == b * TIERS + k, red, stats)
            yield
        f = flux[here, :] * area[here, :]
        for b in range(REGIONS):
            red = jnp.sum(jnp.where(member[b], heat, 0.0), axis=1, keepdims=True)
            stats = jnp.where(lane8 == HEAT + b, red, stats)
            red = jnp.sum(jnp.where(member[b], f, 0.0), axis=1, keepdims=True)
            stats = jnp.where(lane8 == FLUX + b, red, stats)
        stats = jnp.where(lane8 == THETA, jnp.sum(theta_sum, axis=1, keepdims=True), stats)
        stats = jnp.where(lane8 == WET, jnp.sum(wet_sum, axis=1, keepdims=True), stats)
        if south is not None:
            stats = stats + south
        rs_send[g, REGIONS] = stats
        yield

    def bin_rows(hi_r, cl_r, val_r, part_r):
        for jj in range(GROUP):
            total = None
            for k in range(TIERS):
                hi = jnp.broadcast_to(hi_r[k, jj : jj + 1, :], (SIDE, COLS)).astype(BF16)
                cl = jnp.broadcast_to(cl_r[k, jj : jj + 1, :], (SIDE, COLS)).astype(BF16)
                val = jnp.concatenate([val_r[k, half, 8 * jj : 8 * jj + 8, :] for half in range(2)], axis=1)
                val = jnp.concatenate([val] * (SIDE // 8), axis=0).astype(BF16)
                lhs = jnp.where(hi == hi_iota, val, zero)
                rhs = jnp.where(cl == cl_iota, one, zero)
                d = lax.dot_general(lhs, rhs, (((1,), (1,)), ((), ())), preferred_element_type=F32)
                total = d if total is None else total + d
            part_r[pl.ds(jj, SIDE, stride=8), 0:SIDE] = total
            yield

    bin_lane = lax.rem(lane8, LO)
    bin_block = lax.div(lane8, LO)

    def arrange(g, part_r):
        s0 = [jnp.zeros((8, 128), F32)] * REGIONS
        s1 = [jnp.zeros((8, 128), F32)] * REGIONS
        for hi in range(HI):
            rows = [part_r[32 * hi + 8 * n : 32 * hi + 8 * n + 8, :] for n in range(4)]
            wx = rows[2] + rows[3]
            x = rows[0] + rows[1] - wx
            for b in range(REGIONS):
                at = bin_lane + LO * b
                s0[b] = jnp.where(bin_block == hi, jnp.take_along_axis(x, at, axis=1), s0[b])
                s1[b] = jnp.where(bin_block == hi, jnp.take_along_axis(wx, at, axis=1), s1[b])
            yield
        for b in range(REGIONS):
            rs_send[g, b] = s0[b] + jnp.where(lane8 == 0, 0.0, pltpu.roll(s1[b], 1, 1))
        yield

    def together(*parts):
        parts = [p for p in parts if p is not None]
        done = object()
        lead, rest = parts[0], parts[1:]
        per = [2] * len(rest)
        while next(lead, done) is not done:
            for p, n in zip(rest, per):
                for _ in range(n):
                    next(p, done)
        for p in rest:
            while next(p, done) is not done:
                pass

    def send(g):
        for t in range(REGIONS + 1):
            dst, slot = owner(g, t)

            @pl.when(dst != o)
            def _():
                rs_copy(g, t, o).start()

    set_a = (hi_a, cl_a, val_a)
    set_b = (hi_b, cl_b, val_b)

    for load in loads[:3]:
        load.wait()
    flux_totals()
    for load in loads[3:7]:
        load.wait()
    together(prepare(0, *set_a))
    for load in loads[7:]:
        load.wait()
    edge_rows()

    def pair(i, carry):
        g = 2 * i
        together(bin_rows(*set_a, part_a), prepare(g + 1, *set_b), arrange(lax.max(g - 1, 0), part_b))

        @pl.when(i == 0)
        def _():
            first_sends()

        @pl.when(i > 0)
        def _():
            send(g - 1)
        together(bin_rows(*set_b, part_b), prepare(g + 2, *set_a), arrange(g, part_a))
        send(g)
        return carry

    lax.fori_loop(0, 3, pair, 0)
    together(bin_rows(*set_a, part_a), arrange(5, part_b))
    send(5)
    north_row()

    def add_south(q, c):
        return c + jnp.where(q < l, pfx_recv[q], 0.0)

    south = lax.fori_loop(0, NLAT, add_south, jnp.zeros((8, 128), F32))
    together(prepare(7, *set_b, south))
    together(bin_rows(*set_b, part_b), arrange(6, part_a))
    send(6)
    together(arrange(7, part_b))
    send(7)

    b_own, g_low = lax.div(o, 4), lax.rem(o, 4)

    def owned(slot, g, t, scale):
        others(NLON, o, lambda q: pltpu.make_async_remote_copy(
            rs_send.at[0, 0], rs_recv.at[slot, q], rs_ssem.at[0, 0], rs_rsem.at[slot, q],
            device_id={"lon": q}, device_id_type=MESH).wait_recv())
        acc = rs_send[g, t]
        for q in range(NLON):
            acc = acc + jnp.where(q != o, rs_recv[slot, q], 0.0)
        ag_send[slot] = acc * scale

    for slot in (0, 1):
        g = 4 * slot + g_low
        owned(slot, g, b_own, UNIT)
        others(NLON, o, lambda q: class_copy(slot, b_own, g, q).start())
        out_class[b_own, pl.ds(pl.multiple_of(8 * g, 8), 8), :] = ag_send[slot]
    odd = jnp.bitwise_and(o - 2 * b_own - 1, 3)
    g_sum = 2 * b_own + odd

    @pl.when(odd < 2)
    def _():
        owned(2, g_sum, REGIONS, 1.0)
        others(NLON, o, lambda q: sums_copy(g_sum, q).start())
        out_sums[pl.ds(pl.multiple_of(8 * g_sum, 8), 8), :] = ag_send[2]

    for g in range(ROWS // 8):
        for t in range(REGIONS + 1):
            dst, slot = owner(jnp.int32(g), t)

            @pl.when(dst != o)
            def _():
                (class_copy(0, t, g, 0) if t < REGIONS else sums_copy(g, 0)).wait_recv()

    for g in range(ROWS // 8):
        for t in range(REGIONS + 1):
            dst, slot = owner(jnp.int32(g), t)

            @pl.when(dst != o)
            def _():
                rs_copy(g, t, o).wait_send()
    for slot in (0, 1):
        others(NLON, o, lambda q: class_copy(slot, b_own, 4 * slot + g_low, q).wait_send())

    @pl.when(odd < 2)
    def _():
        others(NLON, o, lambda q: sums_copy(g_sum, q).wait_send())

    @pl.when(l > 0)
    def _():
        halo_copy().wait_send()

    @pl.when(l == NLAT - 1)
    def _():
        others(NLON, o, lambda q: fold_copy(q, o).wait_send())

    def north_done(q, c):
        @pl.when(q > l)
        def _():
            pfx_copy(q, l).wait_send()
        return c
    lax.fori_loop(0, NLAT, north_done, 0)


def finish(classes, sums, out_class, out_over, out_heat, out_impl, square):
    out_class[...] = classes[...]
    square[0:ROWS, :] = sums[...]
    square[ROWS:128, :] = jnp.zeros((128 - ROWS, 128), F32)
    flipped = jnp.transpose(square[...])
    lane8 = iota((8, 128), 1)
    sub = iota((TIERS, 128), 0)
    mean = flipped[THETA : THETA + 1, :] / jnp.where(iota((1, 128), 1) < ROWS, flipped[WET : WET + 1, :], 1.0)
    for b in range(REGIONS):
        x = flipped[TIERS * b : TIERS * b + TIERS, :]
        vol = jnp.sum(x, axis=0, keepdims=True)
        res = (UNIT / 16.0) * (flipped[HEAT + b : HEAT + b + 1, :] - vol * mean)
        out_heat[b : b + 1, :] = res[:, 0:ROWS]
        for step in (1, 2, 4, 8):
            x = x + jnp.where(sub >= step, pltpu.roll(x, step, 0), 0.0)
        out_over[b] = (UNIT * x)[:, 0:ROWS]
    c = flipped[FLUX : FLUX + 8, :]
    south = jnp.sum(jnp.where(lane8 == ROWS - 1, c, 0.0), axis=1, keepdims=True)
    for step in (1, 2, 4, 8, 16, 32):
        c = c + jnp.where(lane8 >= step, pltpu.roll(c, step, 1), 0.0)
    out_impl[...] = (IMPLIED * (c[0:4] + south[4:8]))[:, 0:ROWS]


def body(speed, theta, dz, dx, area, flux, tally, region, seam):
    any_ = pl.BlockSpec(memory_space=pltpu.HBM)
    smem = pl.BlockSpec(memory_space=pltpu.SMEM)
    vmem = pl.BlockSpec(memory_space=pltpu.VMEM)
    dma = pltpu.SemaphoreType.DMA
    rows = [pltpu.VMEM((TIERS, GROUP, COLS), F32)] * 2
    sets = (rows + [pltpu.VMEM((TIERS, 2, 8 * GROUP, 128), F32), pltpu.VMEM((8 * SIDE, 128), F32)]) * 2
    classes, sums = pl.pallas_call(
        kernel,
        out_shape=(
            jax.ShapeDtypeStruct((REGIONS, ROWS, BINS), F32),
            jax.ShapeDtypeStruct((ROWS, 128), F32),
        ),
        in_specs=[any_, any_, smem, any_, any_, any_, any_, any_, smem],
        out_specs=(vmem, vmem),
        scratch_shapes=[
            pltpu.VMEM((TIERS, ROWS + 8, COLS), F32),
            pltpu.VMEM((TIERS, ROWS, COLS), F32),
            pltpu.VMEM((ROWS, COLS), F32),
            pltpu.VMEM((ROWS, COLS), F32),
            pltpu.VMEM((ROWS, COLS), F32),
            pltpu.VMEM((ROWS + 8, COLS), jnp.int32),
            pltpu.VMEM((ROWS, COLS), jnp.int32),
            *sets,
            pltpu.VMEM((ROWS // 8, REGIONS + 1, 8, 128), F32),
            pltpu.VMEM((3, NLON, 8, 128), F32),
            pltpu.VMEM((3, 8, 128), F32),
            pltpu.VMEM((24, COLS), F32),
            pltpu.VMEM((24, COLS), F32),
            pltpu.VMEM((24, COLS), F32),
            pltpu.VMEM((NLON, 24, COLS), F32),
            pltpu.VMEM((8, 128), F32),
            pltpu.VMEM((NLAT, 8, 128), F32),
            dma((9,)),
            dma((ROWS // 8, REGIONS + 1)), dma((3, NLON)), dma((3, NLON)),
            dma((REGIONS, ROWS // 8)), dma((ROWS // 8,)),
            dma((NLON,)), dma((NLON,)),
            dma, dma,
            dma((NLAT,)), dma((NLAT,)),
        ],
        compiler_params=pltpu.CompilerParams(collective_id=0, has_side_effects=True, vmem_limit_bytes=VMEM_LIMIT),
    )(speed, theta, dz, dx, area, flux, tally, region, seam)
    out_class, over, heat, impl = pl.pallas_call(
        finish,
        out_shape=(
            jax.ShapeDtypeStruct((REGIONS, ROWS, BINS), F32),
            jax.ShapeDtypeStruct((REGIONS, TIERS, ROWS), F32),
            jax.ShapeDtypeStruct((REGIONS, ROWS), F32),
            jax.ShapeDtypeStruct((REGIONS, ROWS), F32),
        ),
        in_specs=[vmem, vmem],
        out_specs=(vmem,) * 4,
        scratch_shapes=[pltpu.VMEM((128, 128), F32)],
        compiler_params=pltpu.CompilerParams(vmem_limit_bytes=4 * 2**20),
    )(classes, sums)
    return out_class, jnp.transpose(over, (0, 2, 1)), heat, impl


def solution(mesh):
    in_specs = (
        P(None, "lat", "lon"),
        P(None, "lat", "lon"),
        P(),
        P("lat", "lon"),
        P("lat", "lon"),
        P("lat", "lon"),
        P("lat", "lon"),
        P("lat", "lon"),
        P("lon"),
    )
    out_specs = (P(None, "lat", None), P(None, "lat", None), P(None, "lat"), P(None, "lat"))
    return jax.shard_map(body, mesh=mesh, in_specs=in_specs, out_specs=out_specs, check_vma=False)
```

time: 42.4 us -> 34.8 us (0.82)
  Pallas kernels: 38 us -> 32.2 us
  local copies, waits for them, and re-layouts: 3.57 us -> 1.65 us
    pallas_call x1, Pallas kernels: 38 us -> 31.1 us  [body(): pl.pallas_call(kernel, out_shape=(jax.ShapeDtypeStruct((REGIONS, ROWS, BI...]
    pallas_call x1 -> x0, local copies, waits for them, and re-layouts: 1.64 us -> none  [body(): pl.pallas_call(kernel, out_shape=(jax.ShapeDtypeStruct((REGIONS, ROWS, BI...]
    pallas_call x0 -> x1, Pallas kernels: none -> 1.08 us  [body(): pl.pallas_call(finish, out_shape=(jax.ShapeDtypeStruct((REGIONS, ROWS, BI...]
    unnamed x9 -> x4, local copies, waits for them, and re-layouts: 1.93 us -> 1.65 us
where the time goes in v2:
time: 34.8 us; the launch traced here: 34.5 us
  Pallas kernels  32.2 us (93%)
  local copies, waits for them, and re-layouts  1.65 us (5%)
  between operations  0.65 us (2%)
    pallas_call x1, Pallas kernels, body(): pl.pallas_call(kernel, out_shape=(jax.ShapeDtypeStruct((REGIONS, ROWS, BI...  31.1 us
    unnamed x4, local copies, waits for them, and re-layouts  1.65 us
    pallas_call x1, Pallas kernels, body(): pl.pallas_call(finish, out_shape=(jax.ShapeDtypeStruct((REGIONS, ROWS, BI...  1.08 us

profile of v2, /device:TPU:1, one launch (start us, length us, event | category | flops | bytes accessed | tf_op | source)
XLA Modules:
  0.0 34.5 jit_solution(10214082515986282103)
XLA Ops:
  0.6 31.1 %shard_map.120 = (f32[4,64,128]{2,1,0:T(8,128)}, f32[64,128]{1,0:T(8,128)}) custom-call(f32[16,64,256]{2,1,0:T(8,128)} %speed_h.1, f32[16,64,256]{2,1,0:T(8,128)} %theta_h.1, f32[16]{0:T(128)} %dz_s.1, f32[64,256]{1,0:T(8,128)} %dx_h.1, f32[64,256]{1,0:T(8,128)} %area_h.1, f32[64,256]{1,0:T(8,128)} %flux_h.1, s32[64,256]{1,0:T(8,128)} %tally_h.1, ...), custom_call_target="tpu_custom_call" | custom-call | tf_op jit(solution)/shard_map/pallas_call | solution.py:442
  31.8 0.0 copy-start
  31.8 0.9 %copy-done = f32[4,64,128]{2,1,0:T(8,128)S(1)} copy-done((f32[4,64,128]{2,1,0:T(8,128)S(1)}, f32[4,64,128]{2,1,0:T(8,128)}, u32[]{:S(2)}) %copy-start) | copy-done | bytes 131096
  32.7 0.0 copy-start.1
  32.7 0.8 %copy-done.1 = f32[64,128]{1,0:T(8,128)S(1)} copy-done((f32[64,128]{1,0:T(8,128)S(1)}, f32[64,128]{1,0:T(8,128)}, u32[]{:S(2)}) %copy-start.1) | copy-done | bytes 32792
  33.5 1.1 %shard_map.121 = (f32[4,64,128]{2,1,0:T(8,128)}, f32[4,16,64]{2,1,0:T(8,128)}, f32[4,64]{1,0:T(4,128)}, f32[4,64]{1,0:T(4,128)}) custom-call(f32[4,64,128]{2,1,0:T(8,128)S(1)} %copy-done, f32[64,128]{1,0:T(8,128)S(1)} %copy-done.1), custom_call_target="tpu_custom_call" | custom-call | tf_op jit(solution)/shard_map/pallas_call | solution.py:477
Async XLA Ops:
  31.8 0.9 %copy-start = (f32[4,64,128]{2,1,0:T(8,128)S(1)}, f32[4,64,128]{2,1,0:T(8,128)}, u32[]{:S(2)}) copy-start(f32[4,64,128]{2,1,0:T(8,128)} %get-tuple-element.10.classes) | copy-start | bytes 393220
  32.7 0.8 %copy-start.1 = (f32[64,128]{1,0:T(8,128)S(1)}, f32[64,128]{1,0:T(8,128)}, u32[]{:S(2)}) copy-start(f32[64,128]{1,0:T(8,128)} %get-tuple-element.11.sums) | copy-start | bytes 98308

commit v3 on v2

--- a/solution.py
+++ b/solution.py
@@ -24,7 +24,7 @@
 
 UNIT = math.sqrt(BINS / (COLS * NLON * TIERS))
 IMPLIED = 2.0 / math.sqrt(COLS * NLON * ROWS * NLAT)
-VMEM_LIMIT = 66_800_000
+VMEM_LIMIT = 32 * 2**20
 F32, BF16 = jnp.float32, jnp.bfloat16
 
 
@@ -38,9 +38,9 @@
 
 
 def kernel(
-    speed_h, theta_h, dz_s, dx_h, area_h, flux_h, tally_h, region_h, seam_s,
+    speed_h, theta_h, dz_h, dx_h, area_h, flux_h, tally_h, region_h, seam_h,
     out_class, out_sums,
-    th, sp, dx, area, flux, tally, region,
+    th, sp, dx, area, flux, tally, region, dz_s, seam_s,
     hi_a, cl_a, val_a, part_a, hi_b, cl_b, val_b, part_b,
     rs_send, rs_recv, ag_send,
     halo_send, halo_recv, fold_send, fold_recv, pfx_send, pfx_recv,
@@ -59,10 +59,12 @@
         pltpu.make_async_copy(region_h, region, in_sem.at[2]),
         pltpu.make_async_copy(tally_h, tally.at[pl.ds(0, ROWS)], in_sem.at[3]),
         pltpu.make_async_copy(dx_h, dx, in_sem.at[4]),
+        pltpu.make_async_copy(dz_h, dz_s, in_sem.at[9]),
         pltpu.make_async_copy(theta_h.at[:, first], th.at[:, first], in_sem.at[5]),
         pltpu.make_async_copy(speed_h.at[:, first], sp.at[:, first], in_sem.at[6]),
         pltpu.make_async_copy(theta_h.at[:, rest], th.at[:, rest], in_sem.at[7]),
         pltpu.make_async_copy(speed_h.at[:, rest], sp.at[:, rest], in_sem.at[8]),
+        pltpu.make_async_copy(seam_h, seam_s, in_sem.at[10]),
     ]
     for load in loads:
         load.start()
@@ -309,10 +311,10 @@
     for load in loads[:3]:
         load.wait()
     flux_totals()
-    for load in loads[3:7]:
+    for load in loads[3:8]:
         load.wait()
     together(prepare(0, *set_a))
-    for load in loads[7:]:
+    for load in loads[8:]:
         load.wait()
     edge_rows()
 
@@ -434,9 +436,10 @@
 
 def body(speed, theta, dz, dx, area, flux, tally, region, seam):
     any_ = pl.BlockSpec(memory_space=pltpu.HBM)
-    smem = pl.BlockSpec(memory_space=pltpu.SMEM)
     vmem = pl.BlockSpec(memory_space=pltpu.VMEM)
     dma = pltpu.SemaphoreType.DMA
+    inputs = (speed, theta, dz, dx, area, flux, tally, region, seam)
+    inputs = [pltpu.with_memory_space_constraint(x, pltpu.HBM) for x in inputs]
     rows = [pltpu.VMEM((TIERS, GROUP, COLS), F32)] * 2
     sets = (rows + [pltpu.VMEM((TIERS, 2, 8 * GROUP, 128), F32), pltpu.VMEM((8 * SIDE, 128), F32)]) * 2
     classes, sums = pl.pallas_call(
@@ -445,7 +448,7 @@
             jax.ShapeDtypeStruct((REGIONS, ROWS, BINS), F32),
             jax.ShapeDtypeStruct((ROWS, 128), F32),
         ),
-        in_specs=[any_, any_, smem, any_, any_, any_, any_, any_, smem],
+        in_specs=[any_] * 9,
         out_specs=(vmem, vmem),
         scratch_shapes=[
             pltpu.VMEM((TIERS, ROWS + 8, COLS), F32),
@@ -455,6 +458,8 @@
             pltpu.VMEM((ROWS, COLS), F32),
             pltpu.VMEM((ROWS + 8, COLS), jnp.int32),
             pltpu.VMEM((ROWS, COLS), jnp.int32),
+            pltpu.SMEM((TIERS,), F32),
+            pltpu.SMEM((COLS,), jnp.int32),
             *sets,
             pltpu.VMEM((ROWS // 8, REGIONS + 1, 8, 128), F32),
             pltpu.VMEM((3, NLON, 8, 128), F32),
@@ -465,7 +470,7 @@
             pltpu.VMEM((NLON, 24, COLS), F32),
             pltpu.VMEM((8, 128), F32),
             pltpu.VMEM((NLAT, 8, 128), F32),
-            dma((9,)),
+            dma((11,)),
             dma((ROWS // 8, REGIONS + 1)), dma((3, NLON)), dma((3, NLON)),
             dma((REGIONS, ROWS // 8)), dma((ROWS // 8,)),
             dma((NLON,)), dma((NLON,)),
@@ -473,7 +478,7 @@
             dma((NLAT,)), dma((NLAT,)),
         ],
         compiler_params=pltpu.CompilerParams(collective_id=0, has_side_effects=True, vmem_limit_bytes=VMEM_LIMIT),
-    )(speed, theta, dz, dx, area, flux, tally, region, seam)
+    )(*inputs)
     out_class, over, heat, impl = pl.pallas_call(
         finish,
         out_shape=(

time: 34.8 us -> 31.7 us (0.911)
  local copies, waits for them, and re-layouts: 1.65 us -> 0 us
  Pallas kernels: 32.2 us -> 30.9 us
    unnamed x4 -> x0, local copies, waits for them, and re-layouts: 1.65 us -> none
    pallas_call x1, Pallas kernels: 31.1 us -> 29.8 us  [body(): pl.pallas_call(kernel, out_shape=(jax.ShapeDtypeStruct((REGIONS, ROWS, BI...]
where the time goes in v3:
time: 31.7 us; the launch traced here: 31.5 us
  Pallas kernels  30.9 us (97%)
  between operations  0.64 us (2%)
    pallas_call x1, Pallas kernels, body(): pl.pallas_call(kernel, out_shape=(jax.ShapeDtypeStruct((REGIONS, ROWS, BI...  29.8 us
    pallas_call x1, Pallas kernels, body(): pl.pallas_call(finish, out_shape=(jax.ShapeDtypeStruct((REGIONS, ROWS, BI...  1.08 us

profile of v3, /device:TPU:1, one launch (start us, length us, event | category | flops | bytes accessed | tf_op | source)
XLA Modules:
  0.0 31.5 jit_solution(8322185520447421120)
XLA Ops:
  0.6 29.8 %shard_map.120 = (f32[4,64,128]{2,1,0:T(8,128)S(1)}, f32[64,128]{1,0:T(8,128)S(1)}) custom-call(f32[16,64,256]{2,1,0:T(8,128)} %speed_h.1, f32[16,64,256]{2,1,0:T(8,128)} %theta_h.1, f32[16]{0:T(128)} %dz_h.1, f32[64,256]{1,0:T(8,128)} %dx_h.1, f32[64,256]{1,0:T(8,128)} %area_h.1, f32[64,256]{1,0:T(8,128)} %flux_h.1, s32[64,256]{1,0:T(8,128)} %tally_h.1, ...), custom_call_target="tpu_custom_call" | custom-call | tf_op jit(solution)/shard_map/pallas_call | solution.py:445
  30.4 1.1 %shard_map.121 = (f32[4,64,128]{2,1,0:T(8,128)}, f32[4,16,64]{2,1,0:T(8,128)}, f32[4,64]{1,0:T(4,128)}, f32[4,64]{1,0:T(4,128)}) custom-call(f32[4,64,128]{2,1,0:T(8,128)S(1)} %get-tuple-element.10.classes, f32[64,128]{1,0:T(8,128)S(1)} %get-tuple-element.11.sums), custom_call_target="tpu_custom_call" | custom-call | tf_op jit(solution)/shard_map/pallas_call | solution.py:482

commit v4 on v3

--- a/solution.py
+++ b/solution.py
@@ -43,9 +43,9 @@
     th, sp, dx, area, flux, tally, region, dz_s, seam_s,
     hi_a, cl_a, val_a, part_a, hi_b, cl_b, val_b, part_b,
     rs_send, rs_recv, ag_send,
-    halo_send, halo_recv, fold_send, fold_recv, pfx_send, pfx_recv,
+    halo_send, halo_recv, fold_send, fold_recv, own_flux, pair_flux, south_flux, north_flux,
     in_sem, rs_ssem, rs_rsem, ag_ssem, agc_rsem, ags_rsem, fold_ssem, fold_rsem,
-    halo_ssem, halo_rsem, pfx_ssem, pfx_rsem,
+    halo_ssem, halo_rsem, pair_ssem, pair_rsem, chain_ssem, chain_rsem,
 ):
     o = lax.axis_index("lon")
     l = lax.axis_index("lat")
@@ -72,8 +72,11 @@
     barrier = pltpu.get_barrier_semaphore()
     for d in range(1, NLON):
         pl.semaphore_signal(barrier, inc=1, device_id={"lon": lax.rem(o + d, NLON)}, device_id_type=MESH)
-    for d in range(1, NLAT):
-        pl.semaphore_signal(barrier, inc=1, device_id={"lat": lax.rem(l + d, NLAT)}, device_id_type=MESH)
+    near = (-2, -1, 1, 2)
+    for d in near:
+        @pl.when(jnp.logical_and(l + d >= 0, l + d < NLAT))
+        def _():
+            pl.semaphore_signal(barrier, inc=1, device_id={"lat": l + d}, device_id_type=MESH)
 
     def halo_copy():
         return pltpu.make_async_remote_copy(
@@ -84,10 +87,28 @@
             fold_send, fold_recv.at[src], fold_ssem.at[dst], fold_rsem.at[src],
             device_id={"lon": dst}, device_id_type=MESH)
 
-    def pfx_copy(dst, src):
-        return pltpu.make_async_remote_copy(
-            pfx_send, pfx_recv.at[src], pfx_ssem.at[dst], pfx_rsem.at[src],
-            device_id={"lat": dst}, device_id_type=MESH)
+    chip, core = lax.div(l, 2), lax.rem(l, 2)
+
+    def pair_copy():
+        return pltpu.make_async_remote_copy(
+            own_flux, pair_flux, pair_ssem, pair_rsem, device_id={"lat": l + 1 - 2 * core}, device_id_type=MESH)
+
+    def chain_copy():
+        return pltpu.make_async_remote_copy(
+            north_flux, south_flux, chain_ssem, chain_rsem,
+            device_id={"lat": lax.min(l + 2, NLAT - 1)}, device_id_type=MESH)
+
+    def chain_step():
+        pair_copy().wait_recv()
+
+        @pl.when(chip > 0)
+        def _():
+            chain_copy().wait_recv()
+
+        @pl.when(chip < NLAT // 2 - 1)
+        def _():
+            north_flux[...] = south_flux[...] + own_flux[...] + pair_flux[...]
+            chain_copy().start()
 
     def owner(g, t):
         if t < REGIONS:
@@ -130,7 +151,11 @@
         for b in range(REGIONS):
             t = jnp.sum(jnp.sum(acc[b], axis=0, keepdims=True), axis=1, keepdims=True)
             totals = jnp.where(lane8 == SOUTH + b, t, totals)
-        pfx_send[...] = totals
+        own_flux[...] = totals
+
+        @pl.when(chip == 0)
+        def _():
+            south_flux[...] = jnp.zeros((8, 128), F32)
 
     def edge_rows():
         for k in range(TIERS):
@@ -140,7 +165,11 @@
         fold_send[TIERS:24, :] = jnp.broadcast_to(tally[ROWS - 1 : ROWS, :].astype(F32), (8, COLS))
 
     def first_sends():
-        pl.semaphore_wait(barrier, NLON - 1 + NLAT - 1)
+        known = NLON - 1
+        for d in near:
+            known = known + jnp.where(jnp.logical_and(l + d >= 0, l + d < NLAT), 1, 0)
+        pl.semaphore_wait(barrier, known)
+        pair_copy().start()
 
         @pl.when(l == NLAT - 1)
         def _():
@@ -150,13 +179,6 @@
         @pl.when(l > 0)
         def _():
             halo_copy().start()
-
-        def north(q, c):
-            @pl.when(q > l)
-            def _():
-                pfx_copy(q, l).start()
-            return c
-        lax.fori_loop(0, NLAT, north, 0)
 
     def north_row():
         @pl.when(l < NLAT - 1)
@@ -191,20 +213,13 @@
             th[k, ROWS : ROWS + 1, :] = halo_recv[k : k + 1, :]
         tally[ROWS : ROWS + 1, :] = halo_recv[TIERS : TIERS + 1, :].astype(jnp.int32)
 
-        def south(q, c):
-            @pl.when(q < l)
-            def _():
-                pfx_copy(l, q).wait_recv()
-            return c
-        lax.fori_loop(0, NLAT, south, 0)
-
     sub8 = iota((8, COLS), 0)
     hi_iota = lax.shift_right_logical(iota((SIDE, COLS), 0), 2).astype(F32).astype(BF16)
     cl_iota = iota((SIDE, COLS), 0).astype(F32).astype(BF16)
     zero = jnp.zeros((SIDE, COLS), BF16)
     one = jnp.ones((SIDE, COLS), BF16)
 
-    def prepare(g, hi_r, cl_r, val_r, south=None):
+    def prepare(g, hi_r, cl_r, val_r):
         base = g * GROUP if isinstance(g, int) else pl.multiple_of(g * GROUP, GROUP)
         here = pl.ds(base, GROUP)
         nxt = pl.ds(base + GROUP, 1)
@@ -245,8 +260,6 @@
             stats = jnp.where(lane8 == FLUX + b, red, stats)
         stats = jnp.where(lane8 == THETA, jnp.sum(theta_sum, axis=1, keepdims=True), stats)
         stats = jnp.where(lane8 == WET, jnp.sum(wet_sum, axis=1, keepdims=True), stats)
-        if south is not None:
-            stats = stats + south
         rs_send[g, REGIONS] = stats
         yield
 
@@ -326,10 +339,18 @@
         def _():
             first_sends()
 
+        @pl.when(jnp.logical_and(i > 0, chip == 2 * i - 1))
+        def _():
+            chain_step()
+
         @pl.when(i > 0)
         def _():
             send(g - 1)
         together(bin_rows(*set_b, part_b), prepare(g + 2, *set_a), arrange(g, part_a))
+
+        @pl.when(chip == 2 * i)
+        def _():
+            chain_step()
         send(g)
         return carry
 
@@ -338,13 +359,17 @@
     send(5)
     north_row()
 
-    def add_south(q, c):
-        return c + jnp.where(q < l, pfx_recv[q], 0.0)
-
-    south = lax.fori_loop(0, NLAT, add_south, jnp.zeros((8, 128), F32))
-    together(prepare(7, *set_b, south))
+    @pl.when(jnp.logical_or(chip == 5, chip == 6))
+    def _():
+        chain_step()
+    together(prepare(7, *set_b))
     together(bin_rows(*set_b, part_b), arrange(6, part_a))
     send(6)
+
+    @pl.when(chip == 7)
+    def _():
+        chain_step()
+    rs_send[7, REGIONS] = rs_send[7, REGIONS] + south_flux[...] + jnp.where(core == 1, pair_flux[...], 0.0)
     together(arrange(7, part_b))
     send(7)
 
@@ -403,12 +428,11 @@
     def _():
         others(NLON, o, lambda q: fold_copy(q, o).wait_send())
 
-    def north_done(q, c):
-        @pl.when(q > l)
-        def _():
-            pfx_copy(q, l).wait_send()
-        return c
-    lax.fori_loop(0, NLAT, north_done, 0)
+    pair_copy().wait_send()
+
+    @pl.when(chip < NLAT // 2 - 1)
+    def _():
+        chain_copy().wait_send()
 
 
 def finish(classes, sums, out_class, out_over, out_heat, out_impl, square):
@@ -468,14 +492,12 @@
             pltpu.VMEM((24, COLS), F32),
             pltpu.VMEM((24, COLS), F32),
             pltpu.VMEM((NLON, 24, COLS), F32),
-            pltpu.VMEM((8, 128), F32),
-            pltpu.VMEM((NLAT, 8, 128), F32),
+            *([pltpu.VMEM((8, 128), F32)] * 4),
             dma((11,)),
             dma((ROWS // 8, REGIONS + 1)), dma((3, NLON)), dma((3, NLON)),
             dma((REGIONS, ROWS // 8)), dma((ROWS // 8,)),
             dma((NLON,)), dma((NLON,)),
-            dma, dma,
-            dma((NLAT,)), dma((NLAT,)),
+            *([dma] * 6),
         ],
         compiler_params=pltpu.CompilerParams(collective_id=0, has_side_effects=True, vmem_limit_bytes=VMEM_LIMIT),
     )(*inputs)

time: 31.7 us -> 35.3 us (1.11)
  the two profiles are of different devices: /device:TPU:1 before, /device:TPU:224 now
where the time goes in v4:
time: 35.3 us; the launch traced here: 35.1 us
  Pallas kernels  34.5 us (98%)
  between operations  0.64 us (2%)
    pallas_call x1, Pallas kernels, body(): pl.pallas_call(kernel, out_shape=(jax.ShapeDtypeStruct((REGIONS, ROWS, BI...  33.4 us
    pallas_call x1, Pallas kernels, body(): pl.pallas_call(finish, out_shape=(jax.ShapeDtypeStruct((REGIONS, ROWS, BI...  1.08 us

profile of v4, /device:TPU:224, one launch (start us, length us, event | category | flops | bytes accessed | tf_op | source)
XLA Modules:
  0.0 35.1 jit_solution(10340875689694054391)
XLA Ops:
  0.6 33.4 %shard_map.120 = (f32[4,64,128]{2,1,0:T(8,128)S(1)}, f32[64,128]{1,0:T(8,128)S(1)}) custom-call(f32[16,64,256]{2,1,0:T(8,128)} %speed_h.1, f32[16,64,256]{2,1,0:T(8,128)} %theta_h.1, f32[16]{0:T(128)} %dz_h.1, f32[64,256]{1,0:T(8,128)} %dx_h.1, f32[64,256]{1,0:T(8,128)} %area_h.1, f32[64,256]{1,0:T(8,128)} %flux_h.1, s32[64,256]{1,0:T(8,128)} %tally_h.1, ...), custom_call_target="tpu_custom_call" | custom-call | tf_op jit(solution)/shard_map/pallas_call | solution.py:469
  34.1 1.1 %shard_map.121 = (f32[4,64,128]{2,1,0:T(8,128)}, f32[4,16,64]{2,1,0:T(8,128)}, f32[4,64]{1,0:T(4,128)}, f32[4,64]{1,0:T(4,128)}) custom-call(f32[4,64,128]{2,1,0:T(8,128)S(1)} %get-tuple-element.10.classes, f32[64,128]{1,0:T(8,128)S(1)} %get-tuple-element.11.sums), custom_call_target="tpu_custom_call" | custom-call | tf_op jit(solution)/shard_map/pallas_call | solution.py:504

commit v5 on v4

--- a/solution.py
+++ b/solution.py
@@ -43,9 +43,9 @@
     th, sp, dx, area, flux, tally, region, dz_s, seam_s,
     hi_a, cl_a, val_a, part_a, hi_b, cl_b, val_b, part_b,
     rs_send, rs_recv, ag_send,
-    halo_send, halo_recv, fold_send, fold_recv, own_flux, pair_flux, south_flux, north_flux,
+    halo_send, halo_recv, fold_send, fold_recv, own_flux, pair_flux, south_flux, north_flux, offset, offsets,
     in_sem, rs_ssem, rs_rsem, ag_ssem, agc_rsem, ags_rsem, fold_ssem, fold_rsem,
-    halo_ssem, halo_rsem, pair_ssem, pair_rsem, chain_ssem, chain_rsem,
+    halo_ssem, halo_rsem, pair_ssem, pair_rsem, chain_ssem, chain_rsem, off_ssem, off_rsem,
 ):
     o = lax.axis_index("lon")
     l = lax.axis_index("lat")
@@ -93,22 +93,34 @@
         return pltpu.make_async_remote_copy(
             own_flux, pair_flux, pair_ssem, pair_rsem, device_id={"lat": l + 1 - 2 * core}, device_id_type=MESH)
 
+    def down_copy():
+        return pltpu.make_async_remote_copy(
+            south_flux, pair_flux, pair_ssem, pair_rsem, device_id={"lat": l + 1 - 2 * core}, device_id_type=MESH)
+
     def chain_copy():
         return pltpu.make_async_remote_copy(
             north_flux, south_flux, chain_ssem, chain_rsem,
             device_id={"lat": lax.min(l + 2, NLAT - 1)}, device_id_type=MESH)
 
-    def chain_step():
-        pair_copy().wait_recv()
-
-        @pl.when(chip > 0)
-        def _():
-            chain_copy().wait_recv()
-
-        @pl.when(chip < NLAT // 2 - 1)
-        def _():
-            north_flux[...] = south_flux[...] + own_flux[...] + pair_flux[...]
-            chain_copy().start()
+    def offset_copy(dst, src):
+        return pltpu.make_async_remote_copy(
+            offset, offsets.at[src], off_ssem.at[dst], off_rsem.at[src],
+            device_id={"lon": dst}, device_id_type=MESH)
+
+    def chain_step(turn):
+        @pl.when(jnp.logical_and(turn, core == 1))
+        def _():
+            pair_copy().wait_recv()
+
+            @pl.when(chip > 0)
+            def _():
+                chain_copy().wait_recv()
+                down_copy().start()
+
+            @pl.when(chip < NLAT // 2 - 1)
+            def _():
+                north_flux[...] = south_flux[...] + own_flux[...] + pair_flux[...]
+                chain_copy().start()
 
     def owner(g, t):
         if t < REGIONS:
@@ -157,6 +169,10 @@
         def _():
             south_flux[...] = jnp.zeros((8, 128), F32)
 
+            @pl.when(core == 0)
+            def _():
+                pair_flux[...] = jnp.zeros((8, 128), F32)
+
     def edge_rows():
         for k in range(TIERS):
             halo_send[k : k + 1, :] = th[k, 0:1, :]
@@ -169,7 +185,10 @@
         for d in near:
             known = known + jnp.where(jnp.logical_and(l + d >= 0, l + d < NLAT), 1, 0)
         pl.semaphore_wait(barrier, known)
-        pair_copy().start()
+
+        @pl.when(core == 0)
+        def _():
+            pair_copy().start()
 
         @pl.when(l == NLAT - 1)
         def _():
@@ -339,18 +358,14 @@
         def _():
             first_sends()
 
-        @pl.when(jnp.logical_and(i > 0, chip == 2 * i - 1))
-        def _():
-            chain_step()
+        chain_step(jnp.logical_and(i > 0, chip == 2 * i - 1))
 
         @pl.when(i > 0)
         def _():
             send(g - 1)
         together(bin_rows(*set_b, part_b), prepare(g + 2, *set_a), arrange(g, part_a))
 
-        @pl.when(chip == 2 * i)
-        def _():
-            chain_step()
+        chain_step(chip == 2 * i)
         send(g)
         return carry
 
@@ -359,19 +374,21 @@
     send(5)
     north_row()
 
-    @pl.when(jnp.logical_or(chip == 5, chip == 6))
-    def _():
-        chain_step()
+    chain_step(chip == 5)
     together(prepare(7, *set_b))
     together(bin_rows(*set_b, part_b), arrange(6, part_a))
     send(6)
 
-    @pl.when(chip == 7)
-    def _():
-        chain_step()
-    rs_send[7, REGIONS] = rs_send[7, REGIONS] + south_flux[...] + jnp.where(core == 1, pair_flux[...], 0.0)
     together(arrange(7, part_b))
     send(7)
+
+    chain_step(chip >= 6)
+
+    @pl.when(jnp.logical_and(core == 0, chip > 0))
+    def _():
+        down_copy().wait_recv()
+    offset[...] = pair_flux[...] + jnp.where(core == 1, south_flux[...], 0.0)
+    others(NLON, o, lambda q: offset_copy(q, o).start())
 
     b_own, g_low = lax.div(o, 4), lax.rem(o, 4)
 
@@ -406,6 +423,12 @@
             def _():
                 (class_copy(0, t, g, 0) if t < REGIONS else sums_copy(g, 0)).wait_recv()
 
+    others(NLON, o, lambda q: offset_copy(o, q).wait_recv())
+    south = offset[...]
+    for q in range(NLON):
+        south = south + jnp.where(q != o, offsets[q], 0.0)
+    out_sums[ROWS - 8 : ROWS, :] = out_sums[ROWS - 8 : ROWS, :] + south
+
     for g in range(ROWS // 8):
         for t in range(REGIONS + 1):
             dst, slot = owner(jnp.int32(g), t)
@@ -428,9 +451,13 @@
     def _():
         others(NLON, o, lambda q: fold_copy(q, o).wait_send())
 
-    pair_copy().wait_send()
-
-    @pl.when(chip < NLAT // 2 - 1)
+    others(NLON, o, lambda q: offset_copy(q, o).wait_send())
+
+    @pl.when(jnp.logical_or(core == 0, chip > 0))
+    def _():
+        pair_copy().wait_send()
+
+    @pl.when(jnp.logical_and(core == 1, chip < NLAT // 2 - 1))
     def _():
         chain_copy().wait_send()
 
@@ -492,12 +519,13 @@
             pltpu.VMEM((24, COLS), F32),
             pltpu.VMEM((24, COLS), F32),
             pltpu.VMEM((NLON, 24, COLS), F32),
-            *([pltpu.VMEM((8, 128), F32)] * 4),
+            *([pltpu.VMEM((8, 128), F32)] * 5),
+            pltpu.VMEM((NLON, 8, 128), F32),
             dma((11,)),
             dma((ROWS // 8, REGIONS + 1)), dma((3, NLON)), dma((3, NLON)),
             dma((REGIONS, ROWS // 8)), dma((ROWS // 8,)),
             dma((NLON,)), dma((NLON,)),
-            *([dma] * 6),
+            *([dma] * 6), dma((NLON,)), dma((NLON,)),
         ],
         compiler_params=pltpu.CompilerParams(collective_id=0, has_side_effects=True, vmem_limit_bytes=VMEM_LIMIT),
     )(*inputs)

time: 35.3 us -> 29.1 us (0.82)
  Pallas kernels: 34.5 us -> 28.3 us
    pallas_call x1, Pallas kernels: 33.4 us -> 27.3 us  [body(): pl.pallas_call(kernel, out_shape=(jax.ShapeDtypeStruct((REGIONS, ROWS, BI...]
where the time goes in v5:
time: 29.1 us; the launch traced here: 29 us
  Pallas kernels  28.3 us (97%)
  between operations  0.64 us (2%)
    pallas_call x1, Pallas kernels, body(): pl.pallas_call(kernel, out_shape=(jax.ShapeDtypeStruct((REGIONS, ROWS, BI...  27.3 us
    pallas_call x1, Pallas kernels, body(): pl.pallas_call(finish, out_shape=(jax.ShapeDtypeStruct((REGIONS, ROWS, BI...  1.08 us

profile of v5, /device:TPU:224, one launch (start us, length us, event | category | flops | bytes accessed | tf_op | source)
XLA Modules:
  0.0 29.0 jit_solution(16255721528935117451)
XLA Ops:
  0.6 27.3 %shard_map.120 = (f32[4,64,128]{2,1,0:T(8,128)S(1)}, f32[64,128]{1,0:T(8,128)S(1)}) custom-call(f32[16,64,256]{2,1,0:T(8,128)} %speed_h.1, f32[16,64,256]{2,1,0:T(8,128)} %theta_h.1, f32[16]{0:T(128)} %dz_h.1, f32[64,256]{1,0:T(8,128)} %dx_h.1, f32[64,256]{1,0:T(8,128)} %area_h.1, f32[64,256]{1,0:T(8,128)} %flux_h.1, s32[64,256]{1,0:T(8,128)} %tally_h.1, ...), custom_call_target="tpu_custom_call" | custom-call | tf_op jit(solution)/shard_map/pallas_call | solution.py:496
  27.9 1.1 %shard_map.121 = (f32[4,64,128]{2,1,0:T(8,128)}, f32[4,16,64]{2,1,0:T(8,128)}, f32[4,64]{1,0:T(4,128)}, f32[4,64]{1,0:T(4,128)}) custom-call(f32[4,64,128]{2,1,0:T(8,128)S(1)} %get-tuple-element.10.classes, f32[64,128]{1,0:T(8,128)S(1)} %get-tuple-element.11.sums), custom_call_target="tpu_custom_call" | custom-call | tf_op jit(solution)/shard_map/pallas_call | solution.py:532

commit v6 on v5

--- a/solution.py
+++ b/solution.py
@@ -44,7 +44,7 @@
     hi_a, cl_a, val_a, part_a, hi_b, cl_b, val_b, part_b,
     rs_send, rs_recv, ag_send,
     halo_send, halo_recv, fold_send, fold_recv, own_flux, pair_flux, south_flux, north_flux, offset, offsets,
-    in_sem, rs_ssem, rs_rsem, ag_ssem, agc_rsem, ags_rsem, fold_ssem, fold_rsem,
+    in_sem, rs_ssem, rs_rsem, ag_ssem, ag_rsem, fold_ssem, fold_rsem,
     halo_ssem, halo_rsem, pair_ssem, pair_rsem, chain_ssem, chain_rsem, off_ssem, off_rsem,
 ):
     o = lax.axis_index("lon")
@@ -54,14 +54,14 @@
 
     first, rest = pl.ds(0, 16), pl.ds(16, ROWS - 16)
     loads = [
-        pltpu.make_async_copy(flux_h, flux, in_sem.at[0]),
-        pltpu.make_async_copy(area_h, area, in_sem.at[1]),
-        pltpu.make_async_copy(region_h, region, in_sem.at[2]),
         pltpu.make_async_copy(tally_h, tally.at[pl.ds(0, ROWS)], in_sem.at[3]),
         pltpu.make_async_copy(dx_h, dx, in_sem.at[4]),
+        pltpu.make_async_copy(region_h, region, in_sem.at[2]),
         pltpu.make_async_copy(dz_h, dz_s, in_sem.at[9]),
         pltpu.make_async_copy(theta_h.at[:, first], th.at[:, first], in_sem.at[5]),
         pltpu.make_async_copy(speed_h.at[:, first], sp.at[:, first], in_sem.at[6]),
+        pltpu.make_async_copy(flux_h, flux, in_sem.at[0]),
+        pltpu.make_async_copy(area_h, area, in_sem.at[1]),
         pltpu.make_async_copy(theta_h.at[:, rest], th.at[:, rest], in_sem.at[7]),
         pltpu.make_async_copy(speed_h.at[:, rest], sp.at[:, rest], in_sem.at[8]),
         pltpu.make_async_copy(seam_h, seam_s, in_sem.at[10]),
@@ -72,40 +72,40 @@
     barrier = pltpu.get_barrier_semaphore()
     for d in range(1, NLON):
         pl.semaphore_signal(barrier, inc=1, device_id={"lon": lax.rem(o + d, NLON)}, device_id_type=MESH)
-    near = (-2, -1, 1, 2)
-    for d in near:
-        @pl.when(jnp.logical_and(l + d >= 0, l + d < NLAT))
-        def _():
-            pl.semaphore_signal(barrier, inc=1, device_id={"lat": l + d}, device_id_type=MESH)
+    chip, core = lax.div(l, 2), lax.rem(l, 2)
+    sibling = l + 1 - 2 * core
+    for q in range(NLON):
+        pl.semaphore_signal(barrier, inc=1, device_id={"lon": q, "lat": sibling}, device_id_type=MESH)
+    near = (l - 2, l + 2, l - 1 + 2 * core)
+    for n in near:
+        @pl.when(jnp.logical_and(n >= 0, n < NLAT))
+        def _():
+            pl.semaphore_signal(barrier, inc=1, device_id={"lat": n}, device_id_type=MESH)
 
     def halo_copy():
         return pltpu.make_async_remote_copy(
             halo_send, halo_recv, halo_ssem, halo_rsem, device_id={"lat": lax.max(l - 1, 0)}, device_id_type=MESH)
 
-    def fold_copy(dst, src):
-        return pltpu.make_async_remote_copy(
-            fold_send, fold_recv.at[src], fold_ssem.at[dst], fold_rsem.at[src],
-            device_id={"lon": dst}, device_id_type=MESH)
-
-    chip, core = lax.div(l, 2), lax.rem(l, 2)
+    def fold_copy(dst):
+        return pltpu.make_async_remote_copy(
+            fold_send, fold_recv.at[o], fold_ssem, fold_rsem, device_id={"lon": dst}, device_id_type=MESH)
 
     def pair_copy():
         return pltpu.make_async_remote_copy(
-            own_flux, pair_flux, pair_ssem, pair_rsem, device_id={"lat": l + 1 - 2 * core}, device_id_type=MESH)
+            own_flux, pair_flux, pair_ssem, pair_rsem, device_id={"lat": sibling}, device_id_type=MESH)
 
     def down_copy():
         return pltpu.make_async_remote_copy(
-            south_flux, pair_flux, pair_ssem, pair_rsem, device_id={"lat": l + 1 - 2 * core}, device_id_type=MESH)
+            south_flux, pair_flux, pair_ssem, pair_rsem, device_id={"lat": sibling}, device_id_type=MESH)
 
     def chain_copy():
         return pltpu.make_async_remote_copy(
             north_flux, south_flux, chain_ssem, chain_rsem,
             device_id={"lat": lax.min(l + 2, NLAT - 1)}, device_id_type=MESH)
 
-    def offset_copy(dst, src):
-        return pltpu.make_async_remote_copy(
-            offset, offsets.at[src], off_ssem.at[dst], off_rsem.at[src],
-            device_id={"lon": dst}, device_id_type=MESH)
+    def offset_copy(dst):
+        return pltpu.make_async_remote_copy(
+            offset, offsets.at[o], off_ssem, off_rsem, device_id={"lon": dst}, device_id_type=MESH)
 
     def chain_step(turn):
         @pl.when(jnp.logical_and(turn, core == 1))
@@ -127,29 +127,23 @@
             return 4 * t + lax.rem(g, 4), lax.div(g, 4)
         return 4 * lax.div(g, 2) + lax.rem(g + 1, 4), 2
 
-    def rs_copy(g, t, src):
+    def rs_copy(g, t):
         dst, slot = owner(g, t)
         return pltpu.make_async_remote_copy(
-            rs_send.at[g, t], rs_recv.at[slot, src], rs_ssem.at[g, t], rs_rsem.at[slot, src],
-            device_id={"lon": dst}, device_id_type=MESH)
-
-    def class_copy(slot, b, g, dst):
-        return pltpu.make_async_remote_copy(
-            ag_send.at[slot], out_class.at[b, pl.ds(pl.multiple_of(8 * g, 8), 8)],
-            ag_ssem.at[slot, dst], agc_rsem.at[b, g], device_id={"lon": dst}, device_id_type=MESH)
-
-    def sums_copy(g, dst):
-        return pltpu.make_async_remote_copy(
-            ag_send.at[2], out_sums.at[pl.ds(pl.multiple_of(8 * g, 8), 8)],
-            ag_ssem.at[2, dst], ags_rsem.at[g], device_id={"lon": dst}, device_id_type=MESH)
-
-    def others(count, me, act):
-        def step(q, c):
-            @pl.when(q != me)
-            def _():
-                act(q)
-            return c
-        lax.fori_loop(0, count, step, 0)
+            rs_send.at[g, t], rs_recv.at[(3 * core + slot) * NLON + o], rs_ssem, rs_rsem.at[core, slot],
+            device_id={"lon": dst, "lat": 2 * chip + 1}, device_id_type=MESH)
+
+    def remote_tile(g, t):
+        dst, _ = owner(g, t)
+        return jnp.logical_or(core == 0, dst != o)
+
+    steps = [(dx, dy) for dx in range(4) for dy in range(4)]
+    steps.sort(key=lambda d: -(min(d[0], 4 - d[0]) + min(d[1], 4 - d[1])))
+    b_own, g_low = lax.div(o, 4), lax.rem(o, 4)
+    peers = [4 * lax.rem(b_own + dx, 4) + lax.rem(g_low + dy, 4) for dx, dy in steps]
+
+    def landed(ref, sem):
+        pltpu.make_async_copy(ref, ref, sem).wait()
 
     def flux_totals():
         acc = [jnp.zeros((8, COLS), F32) for _ in range(REGIONS)]
@@ -181,9 +175,9 @@
         fold_send[TIERS:24, :] = jnp.broadcast_to(tally[ROWS - 1 : ROWS, :].astype(F32), (8, COLS))
 
     def first_sends():
-        known = NLON - 1
-        for d in near:
-            known = known + jnp.where(jnp.logical_and(l + d >= 0, l + d < NLAT), 1, 0)
+        known = 2 * NLON - 1
+        for n in near:
+            known = known + jnp.where(jnp.logical_and(n >= 0, n < NLAT), 1, 0)
         pl.semaphore_wait(barrier, known)
 
         @pl.when(core == 0)
@@ -192,7 +186,8 @@
 
         @pl.when(l == NLAT - 1)
         def _():
-            others(NLON, o, lambda q: fold_copy(q, o).start())
+            for q in peers[:-1]:
+                fold_copy(q).start()
             fold_recv[o] = fold_send[...]
 
         @pl.when(l > 0)
@@ -206,7 +201,7 @@
 
         @pl.when(l == NLAT - 1)
         def _():
-            others(NLON, o, lambda q: fold_copy(o, q).wait_recv())
+            landed(fold_recv.at[pl.ds(0, NLON - 1)], fold_rsem)
             first = seam_s[0]
             source = lax.shift_right_logical(first, 8)
             at = jnp.bitwise_and(first, COLS - 1)
@@ -331,20 +326,16 @@
 
     def send(g):
         for t in range(REGIONS + 1):
-            dst, slot = owner(g, t)
-
-            @pl.when(dst != o)
+            @pl.when(remote_tile(g, t))
             def _():
-                rs_copy(g, t, o).start()
+                rs_copy(g, t).start()
 
     set_a = (hi_a, cl_a, val_a)
     set_b = (hi_b, cl_b, val_b)
 
-    for load in loads[:3]:
+    for load in loads[:8]:
         load.wait()
     flux_totals()
-    for load in loads[3:8]:
-        load.wait()
     together(prepare(0, *set_a))
     for load in loads[8:]:
         load.wait()
@@ -388,82 +379,109 @@
     def _():
         down_copy().wait_recv()
     offset[...] = pair_flux[...] + jnp.where(core == 1, south_flux[...], 0.0)
-    others(NLON, o, lambda q: offset_copy(q, o).start())
-
-    b_own, g_low = lax.div(o, 4), lax.rem(o, 4)
-
-    def owned(slot, g, t, scale):
-        others(NLON, o, lambda q: pltpu.make_async_remote_copy(
-            rs_send.at[0, 0], rs_recv.at[slot, q], rs_ssem.at[0, 0], rs_rsem.at[slot, q],
-            device_id={"lon": q}, device_id_type=MESH).wait_recv())
-        acc = rs_send[g, t]
-        for q in range(NLON):
-            acc = acc + jnp.where(q != o, rs_recv[slot, q], 0.0)
-        ag_send[slot] = acc * scale
-
-    for slot in (0, 1):
-        g = 4 * slot + g_low
-        owned(slot, g, b_own, UNIT)
-        others(NLON, o, lambda q: class_copy(slot, b_own, g, q).start())
-        out_class[b_own, pl.ds(pl.multiple_of(8 * g, 8), 8), :] = ag_send[slot]
+    for q in peers[:-1]:
+        offset_copy(q).start()
+
+    tiles = NLON * 2 + NLON // 2
+
+    def owned(slot, g, t, scale, put):
+        for c in (0, 1):
+            at = 3 * c + slot
+            landed(rs_recv.at[pl.ds(0, NLON - c)], rs_rsem.at[c, slot])
+            parts = [rs_recv[at * NLON + q] for q in range(NLON)]
+            if c == 1:
+                parts = [jnp.where(q != o, p, 0.0) for q, p in enumerate(parts)] + [rs_send[g, t]]
+            while len(parts) > 1:
+                parts = [sum(parts[i : i + 2]) for i in range(0, len(parts), 2)]
+            ag_send[at] = parts[0] * scale
+            to = put(slot, g)
+            for q in peers[: NLON - c]:
+                pltpu.make_async_remote_copy(
+                    ag_send.at[at], to, ag_ssem, ag_rsem,
+                    device_id={"lon": q, "lat": 2 * chip + c}, device_id_type=MESH).start()
+        to[...] = ag_send[at]
+
+    def put_class(slot, g):
+        return out_class.at[b_own, pl.ds(pl.multiple_of(8 * g, 8), 8)]
+
+    def put_sums(slot, g):
+        return out_sums.at[pl.ds(pl.multiple_of(8 * g, 8), 8)]
+
     odd = jnp.bitwise_and(o - 2 * b_own - 1, 3)
     g_sum = 2 * b_own + odd
 
-    @pl.when(odd < 2)
-    def _():
-        owned(2, g_sum, REGIONS, 1.0)
-        others(NLON, o, lambda q: sums_copy(g_sum, q).start())
-        out_sums[pl.ds(pl.multiple_of(8 * g_sum, 8), 8), :] = ag_send[2]
-
-    for g in range(ROWS // 8):
-        for t in range(REGIONS + 1):
-            dst, slot = owner(jnp.int32(g), t)
-
-            @pl.when(dst != o)
-            def _():
-                (class_copy(0, t, g, 0) if t < REGIONS else sums_copy(g, 0)).wait_recv()
-
-    others(NLON, o, lambda q: offset_copy(o, q).wait_recv())
+    @pl.when(core == 1)
+    def _():
+        owned(0, g_low, b_own, UNIT, put_class)
+
+        @pl.when(jnp.logical_and(odd < 2, g_sum < 7))
+        def _():
+            owned(2, g_sum, REGIONS, 1.0, put_sums)
+        owned(1, 4 + g_low, b_own, UNIT, put_class)
+
+        @pl.when(jnp.logical_and(odd < 2, g_sum == 7))
+        def _():
+            owned(2, g_sum, REGIONS, 1.0, put_sums)
+
+    @pl.when(core == 0)
+    def _():
+        landed(rs_recv.at[pl.ds(0, tiles)], rs_ssem)
+        pair_copy().wait_send()
+
+    @pl.when(core == 1)
+    def _():
+        @pl.when(odd < 2)
+        def _():
+            landed(rs_recv.at[pl.ds(0, tiles - 3)], rs_ssem)
+            landed(rs_recv.at[pl.ds(0, 3 * (2 * NLON - 1))], ag_ssem)
+
+        @pl.when(odd >= 2)
+        def _():
+            landed(rs_recv.at[pl.ds(0, tiles - 2)], rs_ssem)
+            landed(rs_recv.at[pl.ds(0, 2 * (2 * NLON - 1))], ag_ssem)
+
+        @pl.when(chip > 0)
+        def _():
+            pair_copy().wait_send()
+
+        @pl.when(chip < NLAT // 2 - 1)
+        def _():
+            chain_copy().wait_send()
+
+    landed(rs_recv.at[pl.ds(0, NLON - 1)], off_ssem)
+
+    @pl.when(l > 0)
+    def _():
+        halo_copy().wait_send()
+
+    @pl.when(l == NLAT - 1)
+    def _():
+        landed(fold_recv.at[pl.ds(0, NLON - 1)], fold_ssem)
+
+    landed(offsets.at[pl.ds(0, NLON - 1)], off_rsem)
     south = offset[...]
     for q in range(NLON):
         south = south + jnp.where(q != o, offsets[q], 0.0)
+
+    @pl.when(core == 0)
+    def _():
+        landed(rs_recv.at[pl.ds(0, tiles)], ag_rsem)
+
+    @pl.when(core == 1)
+    def _():
+        @pl.when(odd < 2)
+        def _():
+            landed(rs_recv.at[pl.ds(0, tiles - 3)], ag_rsem)
+
+        @pl.when(odd >= 2)
+        def _():
+            landed(rs_recv.at[pl.ds(0, tiles - 2)], ag_rsem)
     out_sums[ROWS - 8 : ROWS, :] = out_sums[ROWS - 8 : ROWS, :] + south
 
-    for g in range(ROWS // 8):
-        for t in range(REGIONS + 1):
-            dst, slot = owner(jnp.int32(g), t)
-
-            @pl.when(dst != o)
-            def _():
-                rs_copy(g, t, o).wait_send()
-    for slot in (0, 1):
-        others(NLON, o, lambda q: class_copy(slot, b_own, 4 * slot + g_low, q).wait_send())
-
-    @pl.when(odd < 2)
-    def _():
-        others(NLON, o, lambda q: sums_copy(g_sum, q).wait_send())
-
-    @pl.when(l > 0)
-    def _():
-        halo_copy().wait_send()
-
-    @pl.when(l == NLAT - 1)
-    def _():
-        others(NLON, o, lambda q: fold_copy(q, o).wait_send())
-
-    others(NLON, o, lambda q: offset_copy(q, o).wait_send())
-
-    @pl.when(jnp.logical_or(core == 0, chip > 0))
-    def _():
-        pair_copy().wait_send()
-
-    @pl.when(jnp.logical_and(core == 1, chip < NLAT // 2 - 1))
-    def _():
-        chain_copy().wait_send()
-
-
-def finish(classes, sums, out_class, out_over, out_heat, out_impl, square):
-    out_class[...] = classes[...]
+
+def finish(classes, sums, out_class, out_over, out_heat, out_impl, square, sem):
+    whole = pltpu.make_async_copy(classes, out_class, sem)
+    whole.start()
     square[0:ROWS, :] = sums[...]
     square[ROWS:128, :] = jnp.zeros((128 - ROWS, 128), F32)
     flipped = jnp.transpose(square[...])
@@ -483,6 +501,7 @@
     for step in (1, 2, 4, 8, 16, 32):
         c = c + jnp.where(lane8 >= step, pltpu.roll(c, step, 1), 0.0)
     out_impl[...] = (IMPLIED * (c[0:4] + south[4:8]))[:, 0:ROWS]
+    whole.wait()
 
 
 def body(speed, theta, dz, dx, area, flux, tally, region, seam):
@@ -513,8 +532,8 @@
             pltpu.SMEM((COLS,), jnp.int32),
             *sets,
             pltpu.VMEM((ROWS // 8, REGIONS + 1, 8, 128), F32),
-            pltpu.VMEM((3, NLON, 8, 128), F32),
-            pltpu.VMEM((3, 8, 128), F32),
+            pltpu.VMEM((2 * 3 * NLON, 8, 128), F32),
+            pltpu.VMEM((2 * 3, 8, 128), F32),
             pltpu.VMEM((24, COLS), F32),
             pltpu.VMEM((24, COLS), F32),
             pltpu.VMEM((24, COLS), F32),
@@ -522,10 +541,9 @@
             *([pltpu.VMEM((8, 128), F32)] * 5),
             pltpu.VMEM((NLON, 8, 128), F32),
             dma((11,)),
-            dma((ROWS // 8, REGIONS + 1)), dma((3, NLON)), dma((3, NLON)),
-            dma((REGIONS, ROWS // 8)), dma((ROWS // 8,)),
-            dma((NLON,)), dma((NLON,)),
-            *([dma] * 6), dma((NLON,)), dma((NLON,)),
+            dma, dma((2, 3)), dma, dma,
+            dma, dma,
+            *([dma] * 8),
         ],
         compiler_params=pltpu.CompilerParams(collective_id=0, has_side_effects=True, vmem_limit_bytes=VMEM_LIMIT),
     )(*inputs)
@@ -538,8 +556,8 @@
             jax.ShapeDtypeStruct((REGIONS, ROWS), F32),
         ),
         in_specs=[vmem, vmem],
-        out_specs=(vmem,) * 4,
-        scratch_shapes=[pltpu.VMEM((128, 128), F32)],
+        out_specs=(any_, vmem, vmem, vmem),
+        scratch_shapes=[pltpu.VMEM((128, 128), F32), dma],
         compiler_params=pltpu.CompilerParams(vmem_limit_bytes=4 * 2**20),
     )(classes, sums)
     return out_class, jnp.transpose(over, (0, 2, 1)), heat, impl

time: 29.1 us -> 27.1 us (0.931)
  the two profiles are of different devices: /device:TPU:224 before, /device:TPU:1 now
where the time goes in v6:
time: 27.1 us; the launch traced here: 27 us
  Pallas kernels  26.3 us (97%)
  between operations  0.64 us (2%)
    pallas_call x1, Pallas kernels, body(): pl.pallas_call(kernel, out_shape=(jax.ShapeDtypeStruct((REGIONS, ROWS, BI...  25.1 us
    pallas_call x1, Pallas kernels, body(): pl.pallas_call(finish, out_shape=(jax.ShapeDtypeStruct((REGIONS, ROWS, BI...  1.29 us

profile of v6, /device:TPU:1, one launch (start us, length us, event | category | flops | bytes accessed | tf_op | source)
XLA Modules:
  0.0 27.0 jit_solution(1248408185523632533)
XLA Ops:
  0.6 25.1 %shard_map.120 = (f32[4,64,128]{2,1,0:T(8,128)S(1)}, f32[64,128]{1,0:T(8,128)S(1)}) custom-call(f32[16,64,256]{2,1,0:T(8,128)} %speed_h.1, f32[16,64,256]{2,1,0:T(8,128)} %theta_h.1, f32[16]{0:T(128)} %dz_h.1, f32[64,256]{1,0:T(8,128)} %dx_h.1, f32[64,256]{1,0:T(8,128)} %area_h.1, f32[64,256]{1,0:T(8,128)} %flux_h.1, s32[64,256]{1,0:T(8,128)} %tally_h.1, ...), custom_call_target="tpu_custom_call" | custom-call | tf_op jit(solution)/shard_map/pallas_call | solution.py:515
  25.7 1.3 %shard_map.121 = (f32[4,64,128]{2,1,0:T(8,128)}, f32[4,16,64]{2,1,0:T(8,128)}, f32[4,64]{1,0:T(4,128)}, f32[4,64]{1,0:T(4,128)}) custom-call(f32[4,64,128]{2,1,0:T(8,128)S(1)} %get-tuple-element.10.classes, f32[64,128]{1,0:T(8,128)S(1)} %get-tuple-element.11.sums), custom_call_target="tpu_custom_call" | custom-call | tf_op jit(solution)/shard_map/pallas_call | solution.py:550

commit v7 on v6

--- a/solution.py
+++ b/solution.py
@@ -123,9 +123,14 @@
                 chain_copy().start()
 
     def owner(g, t):
-        if t < REGIONS:
-            return 4 * t + lax.rem(g, 4), lax.div(g, 4)
-        return 4 * lax.div(g, 2) + lax.rem(g + 1, 4), 2
+        turn = lax.rem(g, 4)
+        wide_x, wide_y = lax.div(turn, 2), lax.rem(turn, 2)
+        late = lax.div(g, 4)
+        b = t if t < REGIONS else 3 * (1 - late)
+        x, y = (b // 2, b % 2) if t < REGIONS else (1 - late, 1 - late)
+        x = jnp.where(wide_x == 1, 3 * x, 1 + x)
+        y = jnp.where(wide_y == 1, 3 * y, 1 + y)
+        return 4 * x + y, (late if t < REGIONS else 2)
 
     def rs_copy(g, t):
         dst, slot = owner(g, t)
@@ -137,10 +142,20 @@
         dst, _ = owner(g, t)
         return jnp.logical_or(core == 0, dst != o)
 
-    steps = [(dx, dy) for dx in range(4) for dy in range(4)]
-    steps.sort(key=lambda d: -(min(d[0], 4 - d[0]) + min(d[1], 4 - d[1])))
-    b_own, g_low = lax.div(o, 4), lax.rem(o, 4)
-    peers = [4 * lax.rem(b_own + dx, 4) + lax.rem(g_low + dy, 4) for dx, dy in steps]
+    x_own, y_own = lax.div(o, 4), lax.rem(o, 4)
+    wide = [jnp.where(jnp.logical_or(v == 0, v == 3), 1, 0) for v in (x_own, y_own)]
+    turn = 2 * wide[0] + wide[1]
+    b_own = 2 * jnp.where(x_own >= 2, 1, 0) + jnp.where(y_own >= 2, 1, 0)
+    peers = (0, 4, 1, 5, 8, 12, 2, 9, 3, 6, 13, 7, 10, 11, 14, 15)
+
+    def to_peers(act, all_of_them=False):
+        for q in peers:
+            if all_of_them:
+                act(q)
+            else:
+                @pl.when(o != q)
+                def _():
+                    act(q)
 
     def landed(ref, sem):
         pltpu.make_async_copy(ref, ref, sem).wait()
@@ -186,8 +201,7 @@
 
         @pl.when(l == NLAT - 1)
         def _():
-            for q in peers[:-1]:
-                fold_copy(q).start()
+            to_peers(lambda q: fold_copy(q).start())
             fold_recv[o] = fold_send[...]
 
         @pl.when(l > 0)
@@ -379,8 +393,7 @@
     def _():
         down_copy().wait_recv()
     offset[...] = pair_flux[...] + jnp.where(core == 1, south_flux[...], 0.0)
-    for q in peers[:-1]:
-        offset_copy(q).start()
+    to_peers(lambda q: offset_copy(q).start())
 
     tiles = NLON * 2 + NLON // 2
 
@@ -395,10 +408,9 @@
                 parts = [sum(parts[i : i + 2]) for i in range(0, len(parts), 2)]
             ag_send[at] = parts[0] * scale
             to = put(slot, g)
-            for q in peers[: NLON - c]:
-                pltpu.make_async_remote_copy(
-                    ag_send.at[at], to, ag_ssem, ag_rsem,
-                    device_id={"lon": q, "lat": 2 * chip + c}, device_id_type=MESH).start()
+            to_peers(lambda q: pltpu.make_async_remote_copy(
+                ag_send.at[at], to, ag_ssem, ag_rsem,
+                device_id={"lon": q, "lat": 2 * chip + c}, device_id_type=MESH).start(), c == 0)
         to[...] = ag_send[at]
 
     def put_class(slot, g):
@@ -407,19 +419,20 @@
     def put_sums(slot, g):
         return out_sums.at[pl.ds(pl.multiple_of(8 * g, 8), 8)]
 
-    odd = jnp.bitwise_and(o - 2 * b_own - 1, 3)
-    g_sum = 2 * b_own + odd
+    has_sums = jnp.logical_or(b_own == 0, b_own == 3)
+    no_sums = jnp.logical_not(has_sums)
+    g_sum = turn + jnp.where(b_own == 0, 4, 0)
 
     @pl.when(core == 1)
     def _():
-        owned(0, g_low, b_own, UNIT, put_class)
-
-        @pl.when(jnp.logical_and(odd < 2, g_sum < 7))
+        owned(0, turn, b_own, UNIT, put_class)
+
+        @pl.when(jnp.logical_and(has_sums, g_sum < 7))
         def _():
             owned(2, g_sum, REGIONS, 1.0, put_sums)
-        owned(1, 4 + g_low, b_own, UNIT, put_class)
-
-        @pl.when(jnp.logical_and(odd < 2, g_sum == 7))
+        owned(1, 4 + turn, b_own, UNIT, put_class)
+
+        @pl.when(jnp.logical_and(has_sums, g_sum == 7))
         def _():
             owned(2, g_sum, REGIONS, 1.0, put_sums)
 
@@ -430,12 +443,12 @@
 
     @pl.when(core == 1)
     def _():
-        @pl.when(odd < 2)
+        @pl.when(has_sums)
         def _():
             landed(rs_recv.at[pl.ds(0, tiles - 3)], rs_ssem)
             landed(rs_recv.at[pl.ds(0, 3 * (2 * NLON - 1))], ag_ssem)
 
-        @pl.when(odd >= 2)
+        @pl.when(no_sums)
         def _():
             landed(rs_recv.at[pl.ds(0, tiles - 2)], rs_ssem)
             landed(rs_recv.at[pl.ds(0, 2 * (2 * NLON - 1))], ag_ssem)
@@ -469,19 +482,18 @@
 
     @pl.when(core == 1)
     def _():
-        @pl.when(odd < 2)
+        @pl.when(has_sums)
         def _():
             landed(rs_recv.at[pl.ds(0, tiles - 3)], ag_rsem)
 
-        @pl.when(odd >= 2)
+        @pl.when(no_sums)
         def _():
             landed(rs_recv.at[pl.ds(0, tiles - 2)], ag_rsem)
     out_sums[ROWS - 8 : ROWS, :] = out_sums[ROWS - 8 : ROWS, :] + south
 
 
-def finish(classes, sums, out_class, out_over, out_heat, out_impl, square, sem):
-    whole = pltpu.make_async_copy(classes, out_class, sem)
-    whole.start()
+def finish(classes, sums, out_class, out_over, out_heat, out_impl, square):
+    out_class[...] = classes[...]
     square[0:ROWS, :] = sums[...]
     square[ROWS:128, :] = jnp.zeros((128 - ROWS, 128), F32)
     flipped = jnp.transpose(square[...])
@@ -501,7 +513,6 @@
     for step in (1, 2, 4, 8, 16, 32):
         c = c + jnp.where(lane8 >= step, pltpu.roll(c, step, 1), 0.0)
     out_impl[...] = (IMPLIED * (c[0:4] + south[4:8]))[:, 0:ROWS]
-    whole.wait()
 
 
 def body(speed, theta, dz, dx, area, flux, tally, region, seam):
@@ -556,8 +567,8 @@
             jax.ShapeDtypeStruct((REGIONS, ROWS), F32),
         ),
         in_specs=[vmem, vmem],
-        out_specs=(any_, vmem, vmem, vmem),
-        scratch_shapes=[pltpu.VMEM((128, 128), F32), dma],
+        out_specs=(vmem,) * 4,
+        scratch_shapes=[pltpu.VMEM((128, 128), F32)],
         compiler_params=pltpu.CompilerParams(vmem_limit_bytes=4 * 2**20),
     )(classes, sums)
     return out_class, jnp.transpose(over, (0, 2, 1)), heat, impl

time: 27.1 us -> 26.1 us (0.963)
  Pallas kernels: 26.3 us -> 25.3 us
    pallas_call x1, Pallas kernels: 25.1 us -> 24.3 us  [body(): pl.pallas_call(kernel, out_shape=(jax.ShapeDtypeStruct((REGIONS, ROWS, BI...]
where the time goes in v7:
time: 26.1 us; the launch traced here: 26 us
  Pallas kernels  25.3 us (97%)
  between operations  0.64 us (2%)
    pallas_call x1, Pallas kernels, body(): pl.pallas_call(kernel, out_shape=(jax.ShapeDtypeStruct((REGIONS, ROWS, BI...  24.3 us
    pallas_call x1, Pallas kernels, body(): pl.pallas_call(finish, out_shape=(jax.ShapeDtypeStruct((REGIONS, ROWS, BI...  1.08 us

profile of v7, /device:TPU:1, one launch (start us, length us, event | category | flops | bytes accessed | tf_op | source)
XLA Modules:
  0.0 26.0 jit_solution(3799187702171387686)
XLA Ops:
  0.6 24.3 %shard_map.120 = (f32[4,64,128]{2,1,0:T(8,128)S(1)}, f32[64,128]{1,0:T(8,128)S(1)}) custom-call(f32[16,64,256]{2,1,0:T(8,128)} %speed_h.1, f32[16,64,256]{2,1,0:T(8,128)} %theta_h.1, f32[16]{0:T(128)} %dz_h.1, f32[64,256]{1,0:T(8,128)} %dx_h.1, f32[64,256]{1,0:T(8,128)} %area_h.1, f32[64,256]{1,0:T(8,128)} %flux_h.1, s32[64,256]{1,0:T(8,128)} %tally_h.1, ...), custom_call_target="tpu_custom_call" | custom-call | tf_op jit(solution)/shard_map/pallas_call | solution.py:526
  24.9 1.1 %shard_map.121 = (f32[4,64,128]{2,1,0:T(8,128)}, f32[4,16,64]{2,1,0:T(8,128)}, f32[4,64]{1,0:T(4,128)}, f32[4,64]{1,0:T(4,128)}) custom-call(f32[4,64,128]{2,1,0:T(8,128)S(1)} %get-tuple-element.10.classes, f32[64,128]{1,0:T(8,128)S(1)} %get-tuple-element.11.sums), custom_call_target="tpu_custom_call" | custom-call | tf_op jit(solution)/shard_map/pallas_call | solution.py:561

commit v8 on v7

--- a/solution.py
+++ b/solution.py
@@ -52,7 +52,7 @@
     lane8 = iota((8, 128), 1)
     MESH = pl.DeviceIdType.MESH
 
-    first, rest = pl.ds(0, 16), pl.ds(16, ROWS - 16)
+    first, rest = pl.ds(0, 24), pl.ds(24, ROWS - 24)
     loads = [
         pltpu.make_async_copy(tally_h, tally.at[pl.ds(0, ROWS)], in_sem.at[3]),
         pltpu.make_async_copy(dx_h, dx, in_sem.at[4]),
@@ -123,7 +123,7 @@
                 chain_copy().start()
 
     def owner(g, t):
-        turn = lax.rem(g, 4)
+        turn = lax.rem(g if t < REGIONS else g + 3, 4)
         wide_x, wide_y = lax.div(turn, 2), lax.rem(turn, 2)
         late = lax.div(g, 4)
         b = t if t < REGIONS else 3 * (1 - late)
@@ -208,38 +208,38 @@
         def _():
             halo_copy().start()
 
-    def north_row():
-        @pl.when(l < NLAT - 1)
-        def _():
-            halo_copy().wait_recv()
-
-        @pl.when(l == NLAT - 1)
-        def _():
-            landed(fold_recv.at[pl.ds(0, NLON - 1)], fold_rsem)
-            first = seam_s[0]
-            source = lax.shift_right_logical(first, 8)
-            at = jnp.bitwise_and(first, COLS - 1)
-            high = fold_recv[source]
-            low = fold_recv[jnp.bitwise_and(source + NLON - 1, NLON - 1)]
-            for t in range(COLS // 128):
-                i = lane8 + 128 * t
-                spot = jnp.bitwise_and(at - i, COLS - 1)
-                lane = jnp.bitwise_and(spot, 127)
-                for r in range(3):
-                    rows = slice(8 * r, 8 * r + 8)
-                    pick = [
-                        jnp.where(
-                            spot >= 128,
-                            jnp.take_along_axis(src[rows, 128:], lane, axis=1),
-                            jnp.take_along_axis(src[rows, :128], lane, axis=1),
-                        )
-                        for src in (high, low)
-                    ]
-                    halo_recv[rows, 128 * t : 128 * t + 128] = jnp.where(i <= at, pick[0], pick[1])
-
+    def put_north():
         for k in range(TIERS):
             th[k, ROWS : ROWS + 1, :] = halo_recv[k : k + 1, :]
         tally[ROWS : ROWS + 1, :] = halo_recv[TIERS : TIERS + 1, :].astype(jnp.int32)
+
+    def north_row():
+        halo_copy().wait_recv()
+        put_north()
+
+    def fold_row():
+        landed(fold_recv.at[pl.ds(0, NLON - 1)], fold_rsem)
+        first = seam_s[0]
+        source = lax.shift_right_logical(first, 8)
+        at = jnp.bitwise_and(first, COLS - 1)
+        high = fold_recv[source]
+        low = fold_recv[jnp.bitwise_and(source + NLON - 1, NLON - 1)]
+        for t in range(COLS // 128):
+            i = lane8 + 128 * t
+            spot = jnp.bitwise_and(at - i, COLS - 1)
+            lane = jnp.bitwise_and(spot, 127)
+            for r in range(3):
+                rows = slice(8 * r, 8 * r + 8)
+                pick = [
+                    jnp.where(
+                        spot >= 128,
+                        jnp.take_along_axis(src[rows, 128:], lane, axis=1),
+                        jnp.take_along_axis(src[rows, :128], lane, axis=1),
+                    )
+                    for src in (high, low)
+                ]
+                halo_recv[rows, 128 * t : 128 * t + 128] = jnp.where(i <= at, pick[0], pick[1])
+        put_north()
 
     sub8 = iota((8, COLS), 0)
     hi_iota = lax.shift_right_logical(iota((SIDE, COLS), 0), 2).astype(F32).astype(BF16)
@@ -349,11 +349,7 @@
 
     for load in loads[:8]:
         load.wait()
-    flux_totals()
     together(prepare(0, *set_a))
-    for load in loads[8:]:
-        load.wait()
-    edge_rows()
 
     def pair(i, carry):
         g = 2 * i
@@ -361,6 +357,10 @@
 
         @pl.when(i == 0)
         def _():
+            for load in loads[8:]:
+                load.wait()
+            flux_totals()
+            edge_rows()
             first_sends()
 
         chain_step(jnp.logical_and(i > 0, chip == 2 * i - 1))
@@ -375,12 +375,18 @@
         return carry
 
     lax.fori_loop(0, 3, pair, 0)
-    together(bin_rows(*set_a, part_a), arrange(5, part_b))
+    @pl.when(l < NLAT - 1)
+    def _():
+        north_row()
+        together(bin_rows(*set_a, part_a), prepare(7, *set_b), arrange(5, part_b))
+
+    @pl.when(l == NLAT - 1)
+    def _():
+        together(bin_rows(*set_a, part_a), arrange(5, part_b))
+        fold_row()
+        together(prepare(7, *set_b))
     send(5)
-    north_row()
-
     chain_step(chip == 5)
-    together(prepare(7, *set_b))
     together(bin_rows(*set_b, part_b), arrange(6, part_a))
     send(6)
 
@@ -421,7 +427,7 @@
 
     has_sums = jnp.logical_or(b_own == 0, b_own == 3)
     no_sums = jnp.logical_not(has_sums)
-    g_sum = turn + jnp.where(b_own == 0, 4, 0)
+    g_sum = lax.rem(turn + 1, 4) + jnp.where(b_own == 0, 4, 0)
 
     @pl.when(core == 1)
     def _():
@@ -492,27 +498,24 @@
     out_sums[ROWS - 8 : ROWS, :] = out_sums[ROWS - 8 : ROWS, :] + south
 
 
-def finish(classes, sums, out_class, out_over, out_heat, out_impl, square):
+def finish(classes, sums, out_class, out_over, out_heat, out_impl):
     out_class[...] = classes[...]
-    square[0:ROWS, :] = sums[...]
-    square[ROWS:128, :] = jnp.zeros((128 - ROWS, 128), F32)
-    flipped = jnp.transpose(square[...])
-    lane8 = iota((8, 128), 1)
-    sub = iota((TIERS, 128), 0)
-    mean = flipped[THETA : THETA + 1, :] / jnp.where(iota((1, 128), 1) < ROWS, flipped[WET : WET + 1, :], 1.0)
+    row, lane = iota((88, 128), 0), iota((88, 128), 1)
+    upto = (row < HEAT) & (lane <= row) & (lax.div(lane, TIERS) == lax.div(row, TIERS))
+    volume = (row >= HEAT) & (row < HEAT + 4) & (lax.div(lane, TIERS) == row - HEAT)
+    same = (row >= 72) & (lane == row - 8)
+    pick = jnp.where(upto | volume | same, 1.0, 0.0)
+    res = lax.dot_general(
+        pick, sums[...], (((1,), (1,)), ((), ())), precision=lax.Precision.HIGHEST, preferred_element_type=F32)
     for b in range(REGIONS):
-        x = flipped[TIERS * b : TIERS * b + TIERS, :]
-        vol = jnp.sum(x, axis=0, keepdims=True)
-        res = (UNIT / 16.0) * (flipped[HEAT + b : HEAT + b + 1, :] - vol * mean)
-        out_heat[b : b + 1, :] = res[:, 0:ROWS]
-        for step in (1, 2, 4, 8):
-            x = x + jnp.where(sub >= step, pltpu.roll(x, step, 0), 0.0)
-        out_over[b] = (UNIT * x)[:, 0:ROWS]
-    c = flipped[FLUX : FLUX + 8, :]
-    south = jnp.sum(jnp.where(lane8 == ROWS - 1, c, 0.0), axis=1, keepdims=True)
-    for step in (1, 2, 4, 8, 16, 32):
-        c = c + jnp.where(lane8 >= step, pltpu.roll(c, step, 1), 0.0)
-    out_impl[...] = (IMPLIED * (c[0:4] + south[4:8]))[:, 0:ROWS]
+        out_over[b] = UNIT * res[TIERS * b : TIERS * b + TIERS]
+    at = HEAT + 8
+    mean = res[at + 4 : at + 5] / res[at + 5 : at + 6]
+    out_heat[...] = (UNIT / 16.0) * (res[at : at + 4] - res[HEAT : HEAT + 4] * mean)
+    flux = res[FLUX + 8 : FLUX + 16]
+    south_of = jnp.where(iota((ROWS, ROWS), 0) <= iota((ROWS, ROWS), 1), 1.0, 0.0)
+    c = jnp.dot(flux, south_of, precision=lax.Precision.HIGHEST, preferred_element_type=F32)
+    out_impl[...] = IMPLIED * (c[0:4] + flux[4:8, ROWS - 1 : ROWS])
 
 
 def body(speed, theta, dz, dx, area, flux, tally, region, seam):
@@ -568,7 +571,6 @@
         ),
         in_specs=[vmem, vmem],
         out_specs=(vmem,) * 4,
-        scratch_shapes=[pltpu.VMEM((128, 128), F32)],
         compiler_params=pltpu.CompilerParams(vmem_limit_bytes=4 * 2**20),
     )(classes, sums)
     return out_class, jnp.transpose(over, (0, 2, 1)), heat, impl

time: 26.1 us -> 26 us (level)
  no operation moved by 1% of the time
where the time goes in v8:
time: 26 us; the launch traced here: 25.9 us
  Pallas kernels  25.2 us (97%)
  between operations  0.64 us (2%)
    pallas_call x1, Pallas kernels, body(): pl.pallas_call(kernel, out_shape=(jax.ShapeDtypeStruct((REGIONS, ROWS, BI...  24.3 us
    pallas_call x1, Pallas kernels, body(): pl.pallas_call(finish, out_shape=(jax.ShapeDtypeStruct((REGIONS, ROWS, BI...  0.99 us

profile of v8, /device:TPU:1, one launch (start us, length us, event | category | flops | bytes accessed | tf_op | source)
XLA Modules:
  0.0 25.9 jit_solution(17350793265861462880)
XLA Ops:
  0.6 24.3 %shard_map.120 = (f32[4,64,128]{2,1,0:T(8,128)S(1)}, f32[64,128]{1,0:T(8,128)S(1)}) custom-call(f32[16,64,256]{2,1,0:T(8,128)} %speed_h.1, f32[16,64,256]{2,1,0:T(8,128)} %theta_h.1, f32[16]{0:T(128)} %dz_h.1, f32[64,256]{1,0:T(8,128)} %dx_h.1, f32[64,256]{1,0:T(8,128)} %area_h.1, f32[64,256]{1,0:T(8,128)} %flux_h.1, s32[64,256]{1,0:T(8,128)} %tally_h.1, ...), custom_call_target="tpu_custom_call" | custom-call | tf_op jit(solution)/shard_map/pallas_call | solution.py:529
  24.9 1.0 %shard_map.121 = (f32[4,64,128]{2,1,0:T(8,128)}, f32[4,16,64]{2,1,0:T(8,128)}, f32[4,64]{1,0:T(4,128)}, f32[4,64]{1,0:T(4,128)}) custom-call(f32[4,64,128]{2,1,0:T(8,128)S(1)} %get-tuple-element.10.classes, f32[64,128]{1,0:T(8,128)S(1)} %get-tuple-element.11.sums), custom_call_target="tpu_custom_call" | custom-call | tf_op jit(solution)/shard_map/pallas_call | solution.py:564

commit v9 on v8

--- a/solution.py
+++ b/solution.py
@@ -124,12 +124,10 @@
 
     def owner(g, t):
         turn = lax.rem(g if t < REGIONS else g + 3, 4)
-        wide_x, wide_y = lax.div(turn, 2), lax.rem(turn, 2)
         late = lax.div(g, 4)
-        b = t if t < REGIONS else 3 * (1 - late)
-        x, y = (b // 2, b % 2) if t < REGIONS else (1 - late, 1 - late)
-        x = jnp.where(wide_x == 1, 3 * x, 1 + x)
-        y = jnp.where(wide_y == 1, 3 * y, 1 + y)
+        high, low = (t // 2, t % 2) if t < REGIONS else (1 - late, 1 - late)
+        x = high + 2 * (1 - lax.rem(turn, 2))
+        y = jnp.where(turn >= 2, 3 * low, 1 + low)
         return 4 * x + y, (late if t < REGIONS else 2)
 
     def rs_copy(g, t):
@@ -143,9 +141,9 @@
         return jnp.logical_or(core == 0, dst != o)
 
     x_own, y_own = lax.div(o, 4), lax.rem(o, 4)
-    wide = [jnp.where(jnp.logical_or(v == 0, v == 3), 1, 0) for v in (x_own, y_own)]
-    turn = 2 * wide[0] + wide[1]
-    b_own = 2 * jnp.where(x_own >= 2, 1, 0) + jnp.where(y_own >= 2, 1, 0)
+    outer = jnp.where(jnp.logical_or(y_own == 0, y_own == 3), 1, 0)
+    turn = 2 * outer + jnp.where(x_own < 2, 1, 0)
+    b_own = 2 * lax.rem(x_own, 2) + jnp.where(y_own >= 2, 1, 0)
     peers = (0, 4, 1, 5, 8, 12, 2, 9, 3, 6, 13, 7, 10, 11, 14, 15)
 
     def to_peers(act, all_of_them=False):

time: 26 us -> 26.6 us (1.023)
  Pallas kernels: 25.2 us -> 25.8 us
    pallas_call x1, Pallas kernels: 24.3 us -> 24.9 us  [body(): pl.pallas_call(kernel, out_shape=(jax.ShapeDtypeStruct((REGIONS, ROWS, BI...]
where the time goes in v9:
time: 26.6 us; the launch traced here: 26.5 us
  Pallas kernels  25.8 us (97%)
  between operations  0.64 us (2%)
    pallas_call x1, Pallas kernels, body(): pl.pallas_call(kernel, out_shape=(jax.ShapeDtypeStruct((REGIONS, ROWS, BI...  24.9 us
    pallas_call x1, Pallas kernels, body(): pl.pallas_call(finish, out_shape=(jax.ShapeDtypeStruct((REGIONS, ROWS, BI...  0.99 us

profile of v9, /device:TPU:1, one launch (start us, length us, event | category | flops | bytes accessed | tf_op | source)
XLA Modules:
  0.0 26.5 jit_solution(11725566124291021982)
XLA Ops:
  0.6 24.9 %shard_map.120 = (f32[4,64,128]{2,1,0:T(8,128)S(1)}, f32[64,128]{1,0:T(8,128)S(1)}) custom-call(f32[16,64,256]{2,1,0:T(8,128)} %speed_h.1, f32[16,64,256]{2,1,0:T(8,128)} %theta_h.1, f32[16]{0:T(128)} %dz_h.1, f32[64,256]{1,0:T(8,128)} %dx_h.1, f32[64,256]{1,0:T(8,128)} %area_h.1, f32[64,256]{1,0:T(8,128)} %flux_h.1, s32[64,256]{1,0:T(8,128)} %tally_h.1, ...), custom_call_target="tpu_custom_call" | custom-call | tf_op jit(solution)/shard_map/pallas_call | solution.py:527
  25.5 1.0 %shard_map.121 = (f32[4,64,128]{2,1,0:T(8,128)}, f32[4,16,64]{2,1,0:T(8,128)}, f32[4,64]{1,0:T(4,128)}, f32[4,64]{1,0:T(4,128)}) custom-call(f32[4,64,128]{2,1,0:T(8,128)S(1)} %get-tuple-element.10.classes, f32[64,128]{1,0:T(8,128)S(1)} %get-tuple-element.11.sums), custom_call_target="tpu_custom_call" | custom-call | tf_op jit(solution)/shard_map/pallas_call | solution.py:562

commit v10 on v8

--- a/solution.py
+++ b/solution.py
@@ -351,6 +351,8 @@
         load.wait()
     together(prepare(0, *set_a))
 
+    fold_early = (l == NLAT - 1) & (x_own >= 2) & (y_own >= 2)
+
     def pair(i, carry):
         g = 2 * i
         together(bin_rows(*set_a, part_a), prepare(g + 1, *set_b), arrange(lax.max(g - 1, 0), part_b))
@@ -361,16 +363,23 @@
                 load.wait()
             flux_totals()
             edge_rows()
+
+        @pl.when(jnp.logical_and(i == 0, fold_early))
+        def _():
             first_sends()
 
-        chain_step(jnp.logical_and(i > 0, chip == 2 * i - 1))
+        chain_step(jnp.logical_and(i > 0, chip == 2 * i - 2))
 
         @pl.when(i > 0)
         def _():
             send(g - 1)
         together(bin_rows(*set_b, part_b), prepare(g + 2, *set_a), arrange(g, part_a))
 
-        chain_step(chip == 2 * i)
+        @pl.when(jnp.logical_and(i == 0, jnp.logical_not(fold_early)))
+        def _():
+            first_sends()
+
+        chain_step(jnp.logical_and(i > 0, chip == 2 * i - 1))
         send(g)
         return carry
 
@@ -386,10 +395,10 @@
         fold_row()
         together(prepare(7, *set_b))
     send(5)
-    chain_step(chip == 5)
+    chain_step(chip == 4)
     together(bin_rows(*set_b, part_b), arrange(6, part_a))
     send(6)
-
+    chain_step(chip == 5)
     together(arrange(7, part_b))
     send(7)
 

time: 26 us -> 26.6 us (1.023)
  the two profiles are of different devices: /device:TPU:1 before, /device:TPU:225 now
where the time goes in v10:
time: 26.6 us; the launch traced here: 26.5 us
  Pallas kernels  25.8 us (97%)
  between operations  0.64 us (2%)
    pallas_call x1, Pallas kernels, body(): pl.pallas_call(kernel, out_shape=(jax.ShapeDtypeStruct((REGIONS, ROWS, BI...  24.9 us
    pallas_call x1, Pallas kernels, body(): pl.pallas_call(finish, out_shape=(jax.ShapeDtypeStruct((REGIONS, ROWS, BI...  0.99 us

profile of v10, /device:TPU:225, one launch (start us, length us, event | category | flops | bytes accessed | tf_op | source)
XLA Modules:
  0.0 26.5 jit_solution(10976839655715582710)
XLA Ops:
  0.6 24.9 %shard_map.120 = (f32[4,64,128]{2,1,0:T(8,128)S(1)}, f32[64,128]{1,0:T(8,128)S(1)}) custom-call(f32[16,64,256]{2,1,0:T(8,128)} %speed_h.1, f32[16,64,256]{2,1,0:T(8,128)} %theta_h.1, f32[16]{0:T(128)} %dz_h.1, f32[64,256]{1,0:T(8,128)} %dx_h.1, f32[64,256]{1,0:T(8,128)} %area_h.1, f32[64,256]{1,0:T(8,128)} %flux_h.1, s32[64,256]{1,0:T(8,128)} %tally_h.1, ...), custom_call_target="tpu_custom_call" | custom-call | tf_op jit(solution)/shard_map/pallas_call | solution.py:538
  25.5 1.0 %shard_map.121 = (f32[4,64,128]{2,1,0:T(8,128)}, f32[4,16,64]{2,1,0:T(8,128)}, f32[4,64]{1,0:T(4,128)}, f32[4,64]{1,0:T(4,128)}) custom-call(f32[4,64,128]{2,1,0:T(8,128)S(1)} %get-tuple-element.10.classes, f32[64,128]{1,0:T(8,128)S(1)} %get-tuple-element.11.sums), custom_call_target="tpu_custom_call" | custom-call | tf_op jit(solution)/shard_map/pallas_call | solution.py:573

commit v11 on v10

--- a/solution.py
+++ b/solution.py
@@ -43,9 +43,9 @@
     th, sp, dx, area, flux, tally, region, dz_s, seam_s,
     hi_a, cl_a, val_a, part_a, hi_b, cl_b, val_b, part_b,
     rs_send, rs_recv, ag_send,
-    halo_send, halo_recv, fold_send, fold_recv, own_flux, pair_flux, south_flux, north_flux, offset, offsets,
+    halo_send, halo_recv, fold_send, fold_recv, own_flux, pair_flux, south_flux, north_flux, offset, offsets, skipped,
     in_sem, rs_ssem, rs_rsem, ag_ssem, ag_rsem, fold_ssem, fold_rsem,
-    halo_ssem, halo_rsem, pair_ssem, pair_rsem, chain_ssem, chain_rsem, off_ssem, off_rsem,
+    halo_ssem, halo_rsem, pair_ssem, pair_rsem, chain_ssem, chain_rsem, off_ssem, off_rsem, skip_ssem, skip_rsem,
 ):
     o = lax.axis_index("lon")
     l = lax.axis_index("lat")
@@ -76,7 +76,9 @@
     sibling = l + 1 - 2 * core
     for q in range(NLON):
         pl.semaphore_signal(barrier, inc=1, device_id={"lon": q, "lat": sibling}, device_id_type=MESH)
-    near = (l - 2, l + 2, l - 1 + 2 * core)
+    near = [l - 2, l + 2, l - 1 + 2 * core]
+    far = jnp.logical_and(core == 1, chip >= 4)
+    near += [jnp.where(far & (l + d > 8), l + d, -1) for d in (-6, -4, 4, 6)]
     for n in near:
         @pl.when(jnp.logical_and(n >= 0, n < NLAT))
         def _():
@@ -106,6 +108,18 @@
     def offset_copy(dst):
         return pltpu.make_async_remote_copy(
             offset, offsets.at[o], off_ssem, off_rsem, device_id={"lon": dst}, device_id_type=MESH)
+
+    def skip_copy(src, dst):
+        return pltpu.make_async_remote_copy(
+            north_flux, skipped.at[src - 4], skip_ssem.at[dst - 5], skip_rsem.at[src - 4],
+            device_id={"lat": 2 * dst + 1}, device_id_type=MESH)
+
+    def skip_sends(act):
+        for src in (4, 5, 6):
+            for dst in range(src + 1, 8):
+                @pl.when(jnp.logical_and(core == 1, chip == src))
+                def _():
+                    act(skip_copy(src, dst))
 
     def chain_step(turn):
         @pl.when(jnp.logical_and(turn, core == 1))
@@ -116,11 +130,41 @@
             def _():
                 chain_copy().wait_recv()
                 down_copy().start()
-
-            @pl.when(chip < NLAT // 2 - 1)
+            north_flux[...] = south_flux[...] + own_flux[...] + pair_flux[...]
+
+            @pl.when(chip < 4)
             def _():
-                north_flux[...] = south_flux[...] + own_flux[...] + pair_flux[...]
                 chain_copy().start()
+
+            @pl.when(chip == 4)
+            def _():
+                for dst in (5, 6, 7):
+                    skip_copy(4, dst).start()
+
+    def early_step(turn):
+        @pl.when(jnp.logical_and(turn, core == 1))
+        def _():
+            pair_copy().wait_recv()
+            north_flux[...] = own_flux[...] + pair_flux[...]
+            for src in (5, 6):
+                @pl.when(chip == src)
+                def _():
+                    for dst in range(src + 1, 8):
+                        skip_copy(src, dst).start()
+
+    def last_step():
+        @pl.when(jnp.logical_and(chip >= 5, core == 1))
+        def _():
+            @pl.when(chip == 7)
+            def _():
+                pair_copy().wait_recv()
+            south_flux[...] = jnp.zeros((8, 128), F32)
+            for src in (4, 5, 6):
+                @pl.when(chip > src)
+                def _():
+                    skip_copy(src, 7).wait_recv()
+                    south_flux[...] = south_flux[...] + skipped[src - 4]
+            down_copy().start()
 
     def owner(g, t):
         turn = lax.rem(g if t < REGIONS else g + 3, 4)
@@ -380,6 +424,7 @@
             first_sends()
 
         chain_step(jnp.logical_and(i > 0, chip == 2 * i - 1))
+        early_step(jnp.logical_and(i == 1, jnp.logical_or(chip == 5, chip == 6)))
         send(g)
         return carry
 
@@ -398,11 +443,10 @@
     chain_step(chip == 4)
     together(bin_rows(*set_b, part_b), arrange(6, part_a))
     send(6)
-    chain_step(chip == 5)
     together(arrange(7, part_b))
     send(7)
 
-    chain_step(chip >= 6)
+    last_step()
 
     @pl.when(jnp.logical_and(core == 0, chip > 0))
     def _():
@@ -472,9 +516,10 @@
         def _():
             pair_copy().wait_send()
 
-        @pl.when(chip < NLAT // 2 - 1)
+        @pl.when(chip < 4)
         def _():
             chain_copy().wait_send()
+    skip_sends(lambda copy: copy.wait_send())
 
     landed(rs_recv.at[pl.ds(0, NLON - 1)], off_ssem)
 
@@ -563,10 +608,11 @@
             pltpu.VMEM((NLON, 24, COLS), F32),
             *([pltpu.VMEM((8, 128), F32)] * 5),
             pltpu.VMEM((NLON, 8, 128), F32),
+            pltpu.VMEM((3, 8, 128), F32),
             dma((11,)),
             dma, dma((2, 3)), dma, dma,
             dma, dma,
-            *([dma] * 8),
+            *([dma] * 8), dma((3,)), dma((3,)),
         ],
         compiler_params=pltpu.CompilerParams(collective_id=0, has_side_effects=True, vmem_limit_bytes=VMEM_LIMIT),
     )(*inputs)

time: 26.6 us -> 25.2 us (0.947)
  the two profiles are of different devices: /device:TPU:225 before, /device:TPU:1 now
where the time goes in v11:
time: 25.2 us; the launch traced here: 25.1 us
  Pallas kernels  24.4 us (97%)
  between operations  0.64 us (3%)
    pallas_call x1, Pallas kernels, body(): pl.pallas_call(kernel, out_shape=(jax.ShapeDtypeStruct((REGIONS, ROWS, BI...  23.4 us
    pallas_call x1, Pallas kernels, body(): pl.pallas_call(finish, out_shape=(jax.ShapeDtypeStruct((REGIONS, ROWS, BI...  0.99 us

profile of v11, /device:TPU:1, one launch (start us, length us, event | category | flops | bytes accessed | tf_op | source)
XLA Modules:
  0.0 25.1 jit_solution(4935040031190827489)
XLA Ops:
  0.6 23.4 %shard_map.120 = (f32[4,64,128]{2,1,0:T(8,128)S(1)}, f32[64,128]{1,0:T(8,128)S(1)}) custom-call(f32[16,64,256]{2,1,0:T(8,128)} %speed_h.1, f32[16,64,256]{2,1,0:T(8,128)} %theta_h.1, f32[16]{0:T(128)} %dz_h.1, f32[64,256]{1,0:T(8,128)} %dx_h.1, f32[64,256]{1,0:T(8,128)} %area_h.1, f32[64,256]{1,0:T(8,128)} %flux_h.1, s32[64,256]{1,0:T(8,128)} %tally_h.1, ...), custom_call_target="tpu_custom_call" | custom-call | tf_op jit(solution)/shard_map/pallas_call | solution.py:583
  24.1 1.0 %shard_map.121 = (f32[4,64,128]{2,1,0:T(8,128)}, f32[4,16,64]{2,1,0:T(8,128)}, f32[4,64]{1,0:T(4,128)}, f32[4,64]{1,0:T(4,128)}) custom-call(f32[4,64,128]{2,1,0:T(8,128)S(1)} %get-tuple-element.10.classes, f32[64,128]{1,0:T(8,128)S(1)} %get-tuple-element.11.sums), custom_call_target="tpu_custom_call" | custom-call | tf_op jit(solution)/shard_map/pallas_call | solution.py:619

commit v12 on v11

--- a/solution.py
+++ b/solution.py
@@ -457,7 +457,7 @@
     tiles = NLON * 2 + NLON // 2
 
     def owned(slot, g, t, scale, put):
-        for c in (0, 1):
+        for c in (1, 0):
             at = 3 * c + slot
             landed(rs_recv.at[pl.ds(0, NLON - c)], rs_rsem.at[c, slot])
             parts = [rs_recv[at * NLON + q] for q in range(NLON)]
@@ -470,7 +470,8 @@
             to_peers(lambda q: pltpu.make_async_remote_copy(
                 ag_send.at[at], to, ag_ssem, ag_rsem,
                 device_id={"lon": q, "lat": 2 * chip + c}, device_id_type=MESH).start(), c == 0)
-        to[...] = ag_send[at]
+            if c == 1:
+                to[...] = ag_send[at]
 
     def put_class(slot, g):
         return out_class.at[b_own, pl.ds(pl.multiple_of(8 * g, 8), 8)]

time: 25.2 us -> 24.4 us (0.968)
  Pallas kernels: 24.4 us -> 23.6 us
    pallas_call x1, Pallas kernels: 23.4 us -> 22.6 us  [body(): pl.pallas_call(kernel, out_shape=(jax.ShapeDtypeStruct((REGIONS, ROWS, BI...]
where the time goes in v12:
time: 24.4 us; the launch traced here: 24.2 us
  Pallas kernels  23.6 us (97%)
  between operations  0.64 us (3%)
    pallas_call x1, Pallas kernels, body(): pl.pallas_call(kernel, out_shape=(jax.ShapeDtypeStruct((REGIONS, ROWS, BI...  22.6 us
    pallas_call x1, Pallas kernels, body(): pl.pallas_call(finish, out_shape=(jax.ShapeDtypeStruct((REGIONS, ROWS, BI...  0.99 us

profile of v12, /device:TPU:1, one launch (start us, length us, event | category | flops | bytes accessed | tf_op | source)
XLA Modules:
  0.0 24.2 jit_solution(12789566289246369643)
XLA Ops:
  0.6 22.6 %shard_map.120 = (f32[4,64,128]{2,1,0:T(8,128)S(1)}, f32[64,128]{1,0:T(8,128)S(1)}) custom-call(f32[16,64,256]{2,1,0:T(8,128)} %speed_h.1, f32[16,64,256]{2,1,0:T(8,128)} %theta_h.1, f32[16]{0:T(128)} %dz_h.1, f32[64,256]{1,0:T(8,128)} %dx_h.1, f32[64,256]{1,0:T(8,128)} %area_h.1, f32[64,256]{1,0:T(8,128)} %flux_h.1, s32[64,256]{1,0:T(8,128)} %tally_h.1, ...), custom_call_target="tpu_custom_call" | custom-call | tf_op jit(solution)/shard_map/pallas_call | solution.py:584
  23.3 1.0 %shard_map.121 = (f32[4,64,128]{2,1,0:T(8,128)}, f32[4,16,64]{2,1,0:T(8,128)}, f32[4,64]{1,0:T(4,128)}, f32[4,64]{1,0:T(4,128)}) custom-call(f32[4,64,128]{2,1,0:T(8,128)S(1)} %get-tuple-element.10.classes, f32[64,128]{1,0:T(8,128)S(1)} %get-tuple-element.11.sums), custom_call_target="tpu_custom_call" | custom-call | tf_op jit(solution)/shard_map/pallas_call | solution.py:620
